TPU v7x, 8 devices: a whole 2x2x1 slice. The times are simulated.
8 devices in a mesh: ens: 1 (over z), col: 2 (over y), row: 4 (over x, core).
Axes of the slice: x: 2, y: 2, z: 1, core: 2. Of those that a mesh axis runs over, the one named last changes fastest.
Arguments:
- u_init: float32 [1024, 1024], P(('ens', 'row'), 'col')
- v_init: float32 [1024, 1024], P(('ens', 'row'), 'col')
- stencil_w: float32 [64, 3, 3], replicated
Outputs:
- output 1: float32 [1024, 1024], P(('ens', 'row'), 'col')
- output 2: float32 [1024, 1024], P(('ens', 'row'), 'col')
All inputs are finite; a program needn't handle non-finite values.
Results may differ from a plain program's by a relative error of at most 0.001.
Values are sent between devices in bfloat16 or wider.
A program may use at most 1 GiB of HBM per device.

v0:
```python
import jax
import jax.numpy as jnp
from jax import lax
from jax.sharding import PartitionSpec as P

TIME_STEP = 0.5


def stencil_valid(block, step_w):
    out_rows = block.shape[0] - 2
    out_cols = block.shape[1] - 2
    total_acc = step_w[0, 0] * block[0:out_rows, 0:out_cols]
    for tap_index in range(1, 9):
        row_off, col_off = divmod(tap_index, 3)
        total_acc = total_acc + step_w[row_off, col_off] * block[row_off:row_off + out_rows, col_off:col_off + out_cols]
    return total_acc


def solution(mesh):
    row_devices = mesh.shape["row"]
    col_devices = mesh.shape["col"]
    row_fwd = [(source_dev, (source_dev + 1) % row_devices) for source_dev in range(row_devices)]
    row_back = [(source_dev, (source_dev - 1) % row_devices) for source_dev in range(row_devices)]
    col_fwd = [(source_dev, (source_dev + 1) % col_devices) for source_dev in range(col_devices)]
    col_back = [(source_dev, (source_dev - 1) % col_devices) for source_dev in range(col_devices)]
    tile_spec = P(("ens", "row"), "col")

    def halo_pad(u_tile):
        from_above = lax.ppermute(u_tile[-1:, :], "row", row_fwd)
        from_below = lax.ppermute(u_tile[:1, :], "row", row_back)
        tall_tile = jnp.concatenate([from_above, u_tile, from_below], axis=0)
        from_left = lax.ppermute(tall_tile[:, -1:], "col", col_fwd)
        from_right = lax.ppermute(tall_tile[:, :1], "col", col_back)
        return jnp.concatenate([from_left, tall_tile, from_right], axis=1)

    def local_run(u_tile, v_tile, stencil_w):
        def one_step(state_pair, step_w):
            u_now, v_now = state_pair
            padded = halo_pad(u_now)
            v_next = v_now + (stencil_valid(padded, step_w) - u_now)
            u_next = u_now + TIME_STEP * v_next
            return (u_next, v_next), None

        (u_final, v_final), _ = lax.scan(one_step, (u_tile, v_tile), stencil_w)
        return u_final, v_final

    return jax.shard_map(local_run, mesh=mesh, in_specs=(tile_spec, tile_spec, P()), out_specs=(tile_spec, tile_spec), check_vma=False)
```

profile of v0, /device:TPU:0, one launch (start us, length us, event | category | flops | bytes accessed | tf_op | source)
XLA Modules:
  0.0 1138.8 jit_solution(13846366587788511599)
XLA Ops:
  1.8 1136.0 %while.12 = (s32[]{:T(128)}, f32[256,512]{1,0:T(8,128)S(1)}, f32[256,512]{1,0:T(8,128)S(1)}, f32[64,3,3]{2,1,0:T(4,128)S(1)}, s32[]{:T(128)}) while((s32[]{:T(128)}, f32[256,512]{1,0:T(8,128)S(1)}, f32[256,512]{1,0:T(8,128)S(1)}, f32[64,3,3]{2,1,0:T(4,128)S(1)}, s32[]{:T(128)}) %tuple.49), condition=%wide.region_1.2_spmd, body=%wide.region_0.1_spmd.sunk | while | flops 3809814 | bytes 8448517 | solution.py:44
  15.5 6.4 multiply_add_fusion.2
  33.6 6.4 multiply_add_fusion.2
  50.9 6.4 multiply_add_fusion.2
  69.0 6.4 multiply_add_fusion.2
  86.3 6.4 multiply_add_fusion.2
  104.4 6.4 multiply_add_fusion.2
  121.7 6.4 multiply_add_fusion.2
  139.9 6.4 multiply_add_fusion.2
  157.1 6.4 multiply_add_fusion.2
  175.3 6.4 multiply_add_fusion.2
  227.9 6.4 multiply_add_fusion.2
  246.1 6.4 multiply_add_fusion.2
  263.4 6.4 multiply_add_fusion.2
  281.5 6.4 multiply_add_fusion.2
  298.8 6.4 multiply_add_fusion.2
  316.9 6.4 multiply_add_fusion.2
  334.2 6.4 multiply_add_fusion.2
  352.3 6.4 multiply_add_fusion.2
  369.6 6.4 multiply_add_fusion.2
  387.7 6.4 multiply_add_fusion.2
  405.0 6.4 multiply_add_fusion.2
  423.2 6.4 multiply_add_fusion.2
  440.4 6.4 multiply_add_fusion.2
  458.6 6.4 multiply_add_fusion.2
  475.8 6.4 multiply_add_fusion.2
  494.0 6.4 multiply_add_fusion.2
  529.4 6.4 multiply_add_fusion.2
  546.7 6.4 multiply_add_fusion.2
  582.1 6.4 multiply_add_fusion.2
  600.2 6.4 multiply_add_fusion.2
  617.5 6.4 multiply_add_fusion.2
  635.6 6.4 multiply_add_fusion.2
  652.9 6.4 multiply_add_fusion.2
  671.1 6.4 multiply_add_fusion.2
  688.3 6.4 multiply_add_fusion.2
  706.5 6.4 multiply_add_fusion.2
  723.7 6.4 multiply_add_fusion.2
  741.9 6.4 multiply_add_fusion.2
  759.1 6.4 multiply_add_fusion.2
  777.3 6.4 multiply_add_fusion.2
  794.6 6.4 multiply_add_fusion.2
  812.7 6.4 multiply_add_fusion.2
  830.0 6.4 multiply_add_fusion.2
  848.1 6.4 multiply_add_fusion.2
  900.8 6.4 multiply_add_fusion.2
  918.9 6.4 multiply_add_fusion.2
  936.2 6.4 multiply_add_fusion.2
  (924 shorter events, 834.2 us)
Async XLA Ops:
  25.1 6.5 collective-permute-start.2
  26.7 6.7 collective-permute-start.3
  60.5 6.5 collective-permute-start.2
  62.1 6.7 collective-permute-start.3
  96.0 6.5 collective-permute-start.2
  97.5 6.7 collective-permute-start.3
  131.4 6.5 collective-permute-start.2
  132.9 6.7 collective-permute-start.3
  166.8 6.5 collective-permute-start.2
  168.3 6.7 collective-permute-start.3
  202.2 6.5 collective-permute-start.2
  203.7 6.7 collective-permute-start.3
  237.6 6.5 collective-permute-start.2
  239.1 6.7 collective-permute-start.3
  273.0 6.5 collective-permute-start.2
  274.6 6.7 collective-permute-start.3
  308.4 6.5 collective-permute-start.2
  310.0 6.7 collective-permute-start.3
  343.8 6.5 collective-permute-start.2
  345.4 6.7 collective-permute-start.3
  380.8 6.7 collective-permute-start.3
  416.2 6.7 collective-permute-start.3
  451.6 6.7 collective-permute-start.3
  485.5 6.5 collective-permute-start.2
  487.0 6.7 collective-permute-start.3
  520.9 6.5 collective-permute-start.2
  522.5 6.7 collective-permute-start.3
  556.3 6.5 collective-permute-start.2
  557.9 6.7 collective-permute-start.3
  593.3 6.7 collective-permute-start.3
  628.7 6.7 collective-permute-start.3
  664.1 6.7 collective-permute-start.3
  699.5 6.7 collective-permute-start.3
  734.9 6.7 collective-permute-start.3
  770.3 6.7 collective-permute-start.3
  805.8 6.7 collective-permute-start.3
  839.6 6.5 collective-permute-start.2
  841.2 6.7 collective-permute-start.3
  875.0 6.5 collective-permute-start.2
  876.6 6.7 collective-permute-start.3
  910.5 6.5 collective-permute-start.2
  912.0 6.7 collective-permute-start.3
  947.4 6.7 collective-permute-start.3
  982.8 6.7 collective-permute-start.3
  1018.2 6.7 collective-permute-start.3
  1053.6 6.7 collective-permute-start.3
  1089.1 6.7 collective-permute-start.3
  1124.5 6.7 collective-permute-start.3
  (213 other events, 763.9 us)
where the time goes:
time: 1140 us
  waiting for transfers between devices  485 us (43%)
  other arithmetic  434 us (38%)
  starting transfers between devices  167 us (15%)
  local copies, waits for them, and re-layouts  48.2 us (4%)
    add x64, other arithmetic, one_step(): u_next = u_now + TIME_STEP * v_next  409 us
    ppermute x64, waiting for transfers between devices, halo_pad(): from_left = lax.ppermute(tall_tile[:, -1:], 'col', col_fwd)  221 us
    ppermute x64, waiting for transfers between devices, halo_pad(): from_above = lax.ppermute(u_tile[-1:, :], 'row', row_fwd)  111 us
    ppermute x64, waiting for transfers between devices, halo_pad(): from_right = lax.ppermute(tall_tile[:, :1], 'col', col_back)  101 us
    ppermute x64, starting transfers between devices, halo_pad(): from_left = lax.ppermute(tall_tile[:, -1:], 'col', col_fwd)  98.6 us
    ppermute x64, waiting for transfers between devices, halo_pad(): from_below = lax.ppermute(u_tile[:1, :], 'row', row_back)  51.8 us
    slice x64, local copies, waits for them, and re-layouts, stencil_valid(): total_acc = step_w[0, 0] * block[0:out_rows, 0:out_cols]  43.4 us
    ppermute x64, starting transfers between devices, halo_pad(): from_right = lax.ppermute(tall_tile[:, :1], 'col', col_back)  32.4 us
  transfers between devices with their start and end apart: 256, of which 256 were waited for; matrix products, arithmetic and copies ran while one was open for 4% of the time, Pallas kernels for 0%

commit v1 on v0

v1 whole, which is shorter than its diff:
```python
import jax
import jax.numpy as jnp
from jax import lax
from jax.experimental import pallas as pl
from jax.experimental.pallas import tpu as pltpu
from jax.sharding import PartitionSpec as P

F32 = jnp.float32
MESH = pl.DeviceIdType.MESH
ROWS, COLS = 256, 512
G = 5
T = 16
SWEEPS = 4
TILES = 3
TILE = (ROWS + 2 * T) // TILES
NG = TILE // 8
OFF = 40
R = OFF + ROWS + OFF


def wave_kernel(u_hbm, v_hbm, w_ref, uo_hbm, vo_hbm, sa, sb, uraw, vraw, pbuf, hbuf, uout, vout, sbuf, rbuf,
                load_sem, raw_ssem, raw_rsem, pk_ssem, pk_rsem, dg_ssem, dg_rsem, ex_ssem, ex_rsem, out_sem):
    row = lax.axis_index("row")
    col = lax.axis_index("col")
    up = lax.rem(row + 3, 4)
    down = lax.rem(row + 1, 4)
    other = 1 - col

    loads = [
        pltpu.make_async_copy(u_hbm, uraw.at[pl.ds(T, ROWS)], load_sem.at[0]),
        pltpu.make_async_copy(v_hbm, vraw.at[pl.ds(T, ROWS)], load_sem.at[1]),
    ]
    for cp in loads:
        cp.start()

    barrier = pltpu.get_barrier_semaphore()
    for rr, cc in ((row, other), (up, col), (down, col), (up, other), (down, other)):
        pl.semaphore_signal(barrier, inc=1, device_id={"row": rr, "col": cc}, device_id_type=MESH)
    pl.semaphore_wait(barrier, 5)

    def raw_copy(f, side):
        src = (u_hbm, v_hbm)[f]
        dst = (uraw, vraw)[f]
        lo, at, to = ((0, T + ROWS, up), (ROWS - T, 0, down))[side]
        return pltpu.make_async_remote_copy(
            src_ref=src.at[pl.ds(lo, T)], dst_ref=dst.at[pl.ds(at, T)],
            send_sem=raw_ssem.at[f, side], recv_sem=raw_rsem.at[f, side],
            device_id={"row": to, "col": col}, device_id_type=MESH)

    raws = [raw_copy(f, side) for side in range(2) for f in range(2)]
    for cp in raws:
        cp.start()

    cuts = [0] + [TILE * (c + 1) - T for c in range(TILES - 1)] + [ROWS]

    def packed_copy(c):
        n = cuts[c + 1] - cuts[c]
        return pltpu.make_async_remote_copy(
            src_ref=pbuf.at[:, pl.ds(cuts[c], n)], dst_ref=hbuf.at[:, pl.ds(T + cuts[c], n)],
            send_sem=pk_ssem.at[c], recv_sem=pk_rsem.at[c],
            device_id={"row": row, "col": other}, device_id_type=MESH)

    def diag_copy(side):
        lo, at, to = ((0, T + ROWS, up), (ROWS - T, 0, down))[side]
        return pltpu.make_async_remote_copy(
            src_ref=pbuf.at[:, pl.ds(lo, T)], dst_ref=hbuf.at[:, pl.ds(at, T)],
            send_sem=dg_ssem.at[side], recv_sem=dg_rsem.at[side],
            device_id={"row": to, "col": other}, device_id_type=MESH)

    packs = [packed_copy(c) for c in range(TILES)]
    diags = [diag_copy(side) for side in range(2)]

    def zero(i, _):
        for g in range(G + 2):
            sa[g, pl.ds(pl.multiple_of(i * 8, 8), 8), :] = jnp.zeros((8, 128), F32)
            sb[g, pl.ds(pl.multiple_of(i * 8, 8), 8), :] = jnp.zeros((8, 128), F32)
        return 0

    lax.fori_loop(0, R // 8, zero, 0)
    for cp in loads:
        cp.wait()

    lane = lax.broadcasted_iota(jnp.int32, (8, 128), 1)

    def pack(i, _):
        r = pl.multiple_of(i * 8, 8)
        for f, ref in ((0, uraw), (1, vraw)):
            pbuf[f, pl.ds(r, 8), :] = jnp.where(lane < 64, ref[pl.ds(r + T, 8), 0:128], ref[pl.ds(r + T, 8), 384:512])
        return 0

    for c in range(TILES):
        lax.fori_loop(cuts[c] // 8, cuts[c + 1] // 8, pack, 0)
        if c == 0:
            diags[0].start()
        packs[c].start()
    diags[1].start()

    def place(g):
        c = lane * G + (g - 64)
        return lax.rem(c + 128, 128), lax.div(c + 128, 128)

    def lanes(x, idx):
        return jnp.take_along_axis(x, idx, axis=1, mode="promise_in_bounds")

    def put_main(i, _):
        r = pl.multiple_of(i * 8, 8)
        q = pl.multiple_of(i * 8 + (OFF - T), 8)
        us = [0.25 * uraw[pl.ds(r, 8), 128 * k:128 * k + 128] for k in range(4)]
        ps = [us[k] - 0.125 * vraw[pl.ds(r, 8), 128 * k:128 * k + 128] for k in range(4)]
        for g in range(G):
            idx, at = place(g)
            for dst, src in ((sa, us), (sb, ps)):
                x = lanes(src[0], idx)
                for k in range(1, 4):
                    x = jnp.where(at == k + 1, lanes(src[k], idx), x)
                dst[g + 1, pl.ds(q, 8), :] = x
        return 0

    def put_halo(i, _):
        r = pl.multiple_of(i * 8, 8)
        q = pl.multiple_of(i * 8 + (OFF - T), 8)
        hu = 0.25 * hbuf[0, pl.ds(r, 8), :]
        hp = hu - 0.125 * hbuf[1, pl.ds(r, 8), :]
        for g in range(G):
            idx, at = place(g)
            out = (at == 0) | (at == 5)
            x = jnp.where(out, lanes(hu, idx), sa[g + 1, pl.ds(q, 8), :])
            sa[g + 1, pl.ds(q, 8), :] = x
            if g == 0:
                sa[G + 1, pl.ds(q, 8), :] = pltpu.roll(x, 127, 1)
            if g == G - 1:
                sa[0, pl.ds(q, 8), :] = pltpu.roll(x, 1, 1)
            sb[g + 1, pl.ds(q, 8), :] = jnp.where(out, lanes(hp, idx), sb[g + 1, pl.ds(q, 8), :])
        return 0

    lax.fori_loop(T // 8, (T + ROWS) // 8, put_main, 0)

    def step(t, src, dst, start):
        wa, wb, wc, wd, we = [0.5 * w_ref[a, b, t] for a, b in ((0, 0), (0, 1), (0, 2), (1, 0), (1, 1))]
        wa, wb, wc, wd, we = [jnp.full((8, 128), x, F32) for x in (wa, wb, wc, wd, 1.5 + we)]
        sv = src.at[:, pl.ds(start - 1, TILE + 2)]
        dv = dst.at[:, pl.ds(start, TILE)]
        for i in range(NG):
            n = [sv[g, pl.ds(8 * i, 8), :] for g in range(G + 2)]
            m = [sv[g, pl.ds(8 * i + 1, 8), :] for g in range(G + 2)]
            s = [sv[g, pl.ds(8 * i + 2, 8), :] for g in range(G + 2)]
            for g in range(1, G + 1):
                x = (wa * (n[g - 1] + s[g + 1]) + wc * (n[g + 1] + s[g - 1])) + (wb * (n[g] + s[g]) + wd * (m[g - 1] + m[g + 1]))
                x = x + (we * m[g] - dv[g, pl.ds(8 * i, 8), :])
                dv[g, pl.ds(8 * i, 8), :] = x
                if g == 1:
                    dv[G + 1, pl.ds(8 * i, 8), :] = pltpu.roll(x, 127, 1)
                if g == G:
                    dv[0, pl.ds(8 * i, 8), :] = pltpu.roll(x, 1, 1)

    def exchange(e, side, to):
        return pltpu.make_async_remote_copy(
            src_ref=sbuf.at[e, side], dst_ref=rbuf.at[e, side],
            send_sem=ex_ssem.at[e, side], recv_sem=ex_rsem.at[e, side],
            device_id={"row": to, "col": col}, device_id_type=MESH)

    def get_plain(i, _):
        r = pl.multiple_of(i * 8, 8)
        q = pl.multiple_of(i * 8 + OFF, 8)
        us = [sa[g + 1, pl.ds(q, 8), :] for g in range(G)]
        vs = [8.0 * (us[g] - sb[g + 1, pl.ds(q, 8), :]) for g in range(G)]
        us = [4.0 * x for x in us]
        for h in range(4):
            p = lane + (128 * h + 64)
            idx, at = lax.div(p, G), lax.rem(p, G)
            for dst, src in ((uout, us), (vout, vs)):
                x = lanes(src[0], idx)
                for g in range(1, G):
                    x = jnp.where(at == g, lanes(src[g], idx), x)
                dst[pl.ds(r, 8), 128 * h:128 * h + 128] = x
        return 0

    ends = [ROWS] + [ROWS + T - TILE * (c + 1) + T for c in range(TILES - 1)] + [0]

    def out_copies(c):
        lo, n = ends[c + 1], ends[c] - ends[c + 1]
        return [pltpu.make_async_copy(src.at[pl.ds(lo, n)], dst.at[pl.ds(lo, n)], out_sem.at[f, c])
                for f, (src, dst) in enumerate(((uout, uo_hbm), (vout, vo_hbm)))]

    def tile(it, _):
        sweep, c = lax.div(it, TILES), lax.rem(it, TILES)
        odd = lax.rem(sweep, 2)
        base = jnp.where(odd == 0, OFF - T + TILE * c, OFF + ROWS + T - TILE * (c + 1))
        sign = 2 * odd - 1

        @pl.when(it == 0)
        def _():
            raws[2].wait_recv()
            raws[3].wait_recv()
            diags[1].wait_recv()
            packs[0].wait_recv()

        @pl.when(it == 1)
        def _():
            packs[1].wait_recv()

        @pl.when(it == 2)
        def _():
            raws[0].wait_recv()
            raws[1].wait_recv()
            diags[0].wait_recv()
            packs[2].wait_recv()

        @pl.when((it == 0) | (it == 2))
        def _():
            at = jnp.where(it == 0, 0, (T + ROWS) // 8)
            lax.fori_loop(at, at + T // 8, put_main, 0)

        @pl.when(sweep == 0)
        def _():
            lax.fori_loop(c * NG, c * NG + NG, put_halo, 0)

        prev = it - 1
        psweep, pc = lax.div(prev, TILES), lax.rem(prev, TILES)
        has_edge = (it > 0) & (pc != 1) & (psweep < SWEEPS - 1)
        pside = jnp.where(pc == 0, lax.rem(psweep, 2), 1 - lax.rem(psweep, 2))

        @pl.when(has_edge)
        def _():
            at = jnp.where(pside == 0, OFF, OFF + ROWS - T)
            for k in range(T // 8):
                q = pl.multiple_of(at + 8 * k, 8)
                for g in range(G):
                    sbuf[psweep, pside, 0, g, pl.ds(8 * k, 8), :] = sa[g + 1, pl.ds(q, 8), :]
                    sbuf[psweep, pside, 1, g, pl.ds(8 * k, 8), :] = sb[g + 1, pl.ds(q, 8), :]

        hside = jnp.where(c == 0, odd, 1 - odd)

        @pl.when((sweep > 0) & (c != 1))
        def _():
            exchange(sweep - 1, 1 - hside, down).wait_recv()
            at = jnp.where(hside == 0, OFF - T, OFF + ROWS)
            for k in range(T // 8):
                q = pl.multiple_of(at + 8 * k, 8)
                for g in range(G):
                    x = rbuf[sweep - 1, 1 - hside, 0, g, pl.ds(8 * k, 8), :]
                    sa[g + 1, pl.ds(q, 8), :] = x
                    if g == 0:
                        sa[G + 1, pl.ds(q, 8), :] = pltpu.roll(x, 127, 1)
                    if g == G - 1:
                        sa[0, pl.ds(q, 8), :] = pltpu.roll(x, 1, 1)
                    sb[g + 1, pl.ds(q, 8), :] = rbuf[sweep - 1, 1 - hside, 1, g, pl.ds(8 * k, 8), :]

        def pair(i, _):
            t = sweep * T + 2 * i
            step(t, sa, sb, base + sign * (2 * i + 1))
            step(t + 1, sb, sa, base + sign * (2 * i + 2))

            @pl.when((i == 0) & has_edge)
            def _():
                exchange(psweep, pside, jnp.where(pside == 0, up, down)).start()

            return 0

        lax.fori_loop(0, T // 2, pair, 0)

        @pl.when(sweep == SWEEPS - 1)
        def _():
            lo = jnp.where(c == TILES - 1, 0, ROWS + 2 * T - TILE * (c + 1))
            hi = jnp.where(c == 0, ROWS, ROWS + 2 * T - TILE * c)
            lax.fori_loop(lax.div(lo, 8), lax.div(hi, 8), get_plain, 0)
            for k in range(TILES):
                @pl.when(c == k)
                def _():
                    for cp in out_copies(k):
                        cp.start()

        return 0

    lax.fori_loop(0, SWEEPS * TILES, tile, 0)

    for cp in raws + packs + diags:
        cp.wait_send()
    for e in range(SWEEPS - 1):
        for side in range(2):
            exchange(e, side, up).wait_send()
    for k in range(TILES):
        for cp in out_copies(k):
            cp.wait()


def solution(mesh):
    def local_run(u_tile, v_tile, w):
        dma = pltpu.SemaphoreType.DMA
        return pl.pallas_call(
            wave_kernel,
            out_shape=[jax.ShapeDtypeStruct((ROWS, COLS), F32)] * 2,
            in_specs=[pl.BlockSpec(memory_space=pl.ANY)] * 2 + [pl.BlockSpec(memory_space=pltpu.SMEM)],
            out_specs=[pl.BlockSpec(memory_space=pl.ANY)] * 2,
            scratch_shapes=[
                pltpu.VMEM((G + 2, R, 128), F32), pltpu.VMEM((G + 2, R, 128), F32),
                pltpu.VMEM((ROWS + 2 * T, COLS), F32), pltpu.VMEM((ROWS + 2 * T, COLS), F32),
                pltpu.VMEM((2, ROWS, 128), F32), pltpu.VMEM((2, ROWS + 2 * T, 128), F32),
                pltpu.VMEM((ROWS, COLS), F32), pltpu.VMEM((ROWS, COLS), F32),
                pltpu.VMEM((SWEEPS - 1, 2, 2, G, T, 128), F32), pltpu.VMEM((SWEEPS - 1, 2, 2, G, T, 128), F32),
                dma((2,)), dma((2, 2)), dma((2, 2)), dma((TILES,)), dma((TILES,)), dma((2,)), dma((2,)),
                dma((SWEEPS - 1, 2)), dma((SWEEPS - 1, 2)), dma((2, TILES)),
            ],
            compiler_params=pltpu.CompilerParams(collective_id=0, has_side_effects=True),
        )(u_tile, v_tile, jnp.transpose(w, (1, 2, 0)))

    tile_spec = P(("ens", "row"), "col")
    return jax.shard_map(local_run, mesh=mesh, in_specs=(tile_spec, tile_spec, P()), out_specs=(tile_spec, tile_spec), check_vma=False)
```

time: 1140 us -> 61 us (0.05)
  the two profiles are of different devices: /device:TPU:0 before, /device:TPU:1 now
where the time goes in v1:
time: 61 us; the launch traced here: 60.8 us
  Pallas kernels  57.5 us (94%)
  local copies, waits for them, and re-layouts  2.72 us (4%)
  between operations  0.65 us (1%)
    pallas_call x1, Pallas kernels, local_run(): pl.pallas_call(wave_kernel, out_shape=[jax.ShapeDtypeStruct((ROWS, COLS),...  57.5 us
    unnamed x4, local copies, waits for them, and re-layouts  2.72 us

profile of v1, /device:TPU:1, one launch (start us, length us, event | category | flops | bytes accessed | tf_op | source)
XLA Modules:
  0.0 60.8 jit_solution(16667680404551150373)
XLA Ops:
  0.6 57.5 %shard_map.50 = (f32[256,512]{1,0:T(8,128)}, f32[256,512]{1,0:T(8,128)}) custom-call(f32[256,512]{1,0:T(8,128)} %u_hbm.1, f32[256,512]{1,0:T(8,128)} %v_hbm.1, f32[3,3,64]{2,1,0:T(4,128)} %bitcast.1), custom_call_target="tpu_custom_call" | custom-call | tf_op jit(solution)/shard_map/pallas_call | solution.py:290
  58.1 0.0 copy-start
  58.1 1.9 %copy.7 = f32[256,512]{1,0:T(8,128)} copy(f32[256,512]{1,0:T(8,128)} %get-tuple-element.4) | data formatting | bytes 1048576
  60.0 0.0 copy-done
  60.0 0.8 %copy.8 = f32[256,512]{1,0:T(8,128)} copy(f32[256,512]{1,0:T(8,128)S(1)} %copy-done) | data formatting | bytes 1048576
Async XLA Ops:
  58.1 1.9 %copy-start = (f32[256,512]{1,0:T(8,128)S(1)}, f32[256,512]{1,0:T(8,128)}, u32[]{:S(2)}) copy-start(f32[256,512]{1,0:T(8,128)} %get-tuple-element.5) | copy-start | bytes 1572868

commit v2 on v1

v2 whole, which is shorter than its diff:
```python
import jax
import jax.numpy as jnp
from jax import lax
from jax.experimental import pallas as pl
from jax.experimental.pallas import tpu as pltpu
from jax.sharding import PartitionSpec as P

F32 = jnp.float32
MESH = pl.DeviceIdType.MESH
ROWS, COLS = 256, 512
G = 5
T = 16
SWEEPS = 4
TILES = 3
TILE = (ROWS + 2 * T) // TILES
NG = TILE // 8
OFF = 40
R = OFF + ROWS + OFF


def wave_kernel(u_hbm, v_hbm, w_hbm, uo_hbm, vo_hbm, st, w_ref, maps, uraw, vraw, pbuf, hbuf, uout, vout, sbuf, rbuf,
                load_sem, raw_ssem, raw_rsem, pk_ssem, pk_rsem, dg_ssem, dg_rsem, ex_ssem, ex_rsem, out_sem):
    row = lax.axis_index("row")
    col = lax.axis_index("col")
    up = lax.rem(row + 3, 4)
    down = lax.rem(row + 1, 4)
    other = 1 - col

    loads = [
        pltpu.make_async_copy(u_hbm, uraw.at[pl.ds(T, ROWS)], load_sem.at[0]),
        pltpu.make_async_copy(v_hbm, vraw.at[pl.ds(T, ROWS)], load_sem.at[1]),
        pltpu.make_async_copy(w_hbm, w_ref, load_sem.at[2]),
    ]
    for cp in loads:
        cp.start()

    barrier = pltpu.get_barrier_semaphore()
    for rr, cc in ((row, other), (up, col), (down, col), (up, other), (down, other)):
        pl.semaphore_signal(barrier, inc=1, device_id={"row": rr, "col": cc}, device_id_type=MESH)
    pl.semaphore_wait(barrier, 5)

    def raw_copy(f, side):
        src = (u_hbm, v_hbm)[f]
        dst = (uraw, vraw)[f]
        lo, at, to = ((0, T + ROWS, up), (ROWS - T, 0, down))[side]
        return pltpu.make_async_remote_copy(
            src_ref=src.at[pl.ds(lo, T)], dst_ref=dst.at[pl.ds(at, T)],
            send_sem=raw_ssem.at[f, side], recv_sem=raw_rsem.at[f, side],
            device_id={"row": to, "col": col}, device_id_type=MESH)

    raws = [raw_copy(f, side) for side in range(2) for f in range(2)]
    for cp in raws[2:] + raws[:2]:
        cp.start()

    cuts = [0] + [TILE * (c + 1) - T for c in range(TILES - 1)] + [ROWS]

    def packed_copy(c):
        n = cuts[c + 1] - cuts[c]
        return pltpu.make_async_remote_copy(
            src_ref=pbuf.at[:, pl.ds(cuts[c], n)], dst_ref=hbuf.at[:, pl.ds(T + cuts[c], n)],
            send_sem=pk_ssem.at[c], recv_sem=pk_rsem.at[c],
            device_id={"row": row, "col": other}, device_id_type=MESH)

    def diag_copy(side):
        lo, at, to = ((0, T + ROWS, up), (ROWS - T, 0, down))[side]
        return pltpu.make_async_remote_copy(
            src_ref=pbuf.at[:, pl.ds(lo, T)], dst_ref=hbuf.at[:, pl.ds(at, T)],
            send_sem=dg_ssem.at[side], recv_sem=dg_rsem.at[side],
            device_id={"row": to, "col": other}, device_id_type=MESH)

    packs = [packed_copy(c) for c in range(TILES)]
    diags = [diag_copy(side) for side in range(2)]

    def zero(i, _):
        for f in range(2):
            for g in range(G + 2):
                st[f, g, pl.ds(pl.multiple_of(i * 8, 8), 8), :] = jnp.zeros((8, 128), F32)
        return 0

    lax.fori_loop(0, (OFF - T) // 8, zero, 0)
    lax.fori_loop((OFF + ROWS + T) // 8, R // 8, zero, 0)

    lane = lax.broadcasted_iota(jnp.int32, (8, 128), 1)
    maps[2 * G] = lax.rem(lane, G)
    for g in range(G):
        maps[g] = lax.rem(lane * G + (g + 64), 128)
        k = lax.rem(3 * (lane + (2 * G - g - 1)), G)
        maps[G + g] = lax.div(lax.rem(128 * k + lane + 64, 128 * G), G)

    for cp in loads:
        cp.wait()

    def pack(i, _):
        r = pl.multiple_of(i * 8, 8)
        for f, ref in ((0, uraw), (1, vraw)):
            pbuf[f, pl.ds(r, 8), :] = jnp.where(lane < 64, ref[pl.ds(r + T, 8), 0:128], ref[pl.ds(r + T, 8), 384:512])
        return 0

    lax.fori_loop((ROWS - T) // 8, ROWS // 8, pack, 0)
    lax.fori_loop(0, cuts[1] // 8, pack, 0)
    diags[1].start()
    packs[0].start()
    diags[0].start()
    lax.fori_loop(cuts[1] // 8, (ROWS - T) // 8, pack, 0)
    packs[1].start()
    packs[2].start()

    def lanes(x, idx):
        return jnp.take_along_axis(x, idx, axis=1, mode="promise_in_bounds")

    UN = 4

    def put(i, _):
        residue = maps[2 * G]
        rows = [(pl.multiple_of((i * UN + n) * 8, 8), pl.multiple_of((i * UN + n) * 8 + (OFF - T), 8)) for n in range(UN)]
        srcs = []
        for r, q in rows:
            us = [0.25 * uraw[pl.ds(r, 8), 128 * k:128 * k + 128] for k in range(4)] + [0.25 * hbuf[0, pl.ds(r, 8), :]]
            vs = [vraw[pl.ds(r, 8), 128 * k:128 * k + 128] for k in range(4)] + [hbuf[1, pl.ds(r, 8), :]]
            srcs.append((us, [u - 0.125 * v for u, v in zip(us, vs)]))
        for g in range(G):
            idx = maps[g]
            for (r, q), pair in zip(rows, srcs):
                for f in range(2):
                    x = pair[f][4]
                    for k in range(4):
                        x = jnp.where(residue == (g + 1 + 2 * k) % G, pair[f][k], x)
                    x = lanes(x, idx)
                    st[f, g + 1, pl.ds(q, 8), :] = x
                    if f == 0 and g == 0:
                        st[0, G + 1, pl.ds(q, 8), :] = pltpu.roll(x, 127, 1)
                    if f == 0 and g == G - 1:
                        st[0, 0, pl.ds(q, 8), :] = pltpu.roll(x, 1, 1)
        return 0

    def step(t, src, start):
        dst = 1 - src
        wa, wb, wc, wd, we = [0.5 * w_ref[a, b, t] for a, b in ((0, 0), (0, 1), (0, 2), (1, 0), (1, 1))]
        wa, wb, wc, wd, we = [jnp.full((8, 128), x, F32) for x in (wa, wb, wc, wd, 1.5 + we)]
        sv = st.at[:, :, pl.ds(start - 1, TILE + 2)]
        for i in range(NG):
            n = [sv[src, g, pl.ds(8 * i, 8), :] for g in range(G + 2)]
            m = [sv[src, g, pl.ds(8 * i + 1, 8), :] for g in range(G + 2)]
            s = [sv[src, g, pl.ds(8 * i + 2, 8), :] for g in range(G + 2)]
            for g in range(1, G + 1):
                x = (wa * (n[g - 1] + s[g + 1]) + wc * (n[g + 1] + s[g - 1])) + (wb * (n[g] + s[g]) + wd * (m[g - 1] + m[g + 1]))
                x = x + (we * m[g] - sv[dst, g, pl.ds(8 * i + 1, 8), :])
                sv[dst, g, pl.ds(8 * i + 1, 8), :] = x
                if g == 1:
                    sv[dst, G + 1, pl.ds(8 * i + 1, 8), :] = pltpu.roll(x, 127, 1)
                if g == G:
                    sv[dst, 0, pl.ds(8 * i + 1, 8), :] = pltpu.roll(x, 1, 1)

    def exchange(e, side, to):
        return pltpu.make_async_remote_copy(
            src_ref=sbuf.at[e, side], dst_ref=rbuf.at[e, side],
            send_sem=ex_ssem.at[e, side], recv_sem=ex_rsem.at[e, side],
            device_id={"row": to, "col": col}, device_id_type=MESH)

    def get_plain(i, _):
        residue = maps[2 * G]
        for f, out in ((0, uout), (1, vout)):
            zs = []
            for n in range(UN):
                q = pl.multiple_of((i * UN + n) * 8 + OFF, 8)
                for g in range(G):
                    x = st[0, g + 1, pl.ds(q, 8), :]
                    zs.append(4.0 * x if f == 0 else 8.0 * (x - st[1, g + 1, pl.ds(q, 8), :]))
            for g in range(G):
                idx = maps[G + g]
                for n in range(UN):
                    zs[n * G + g] = lanes(zs[n * G + g], idx)
            for n in range(UN):
                r = pl.multiple_of((i * UN + n) * 8, 8)
                for k in range(4):
                    x = zs[n * G]
                    for g in range(1, G):
                        x = jnp.where(residue == (g + 1 + 2 * k) % G, zs[n * G + g], x)
                    out[pl.ds(r, 8), 128 * k:128 * k + 128] = x
        return 0

    ends = [ROWS] + [ROWS + T - TILE * (c + 1) + T for c in range(TILES - 1)] + [0]

    def out_copies(c):
        lo, n = ends[c + 1], ends[c] - ends[c + 1]
        return [pltpu.make_async_copy(src.at[pl.ds(lo, n)], dst.at[pl.ds(lo, n)], out_sem.at[f, c])
                for f, (src, dst) in enumerate(((uout, uo_hbm), (vout, vo_hbm)))]

    def tile(it, _):
        sweep, c = lax.div(it, TILES), lax.rem(it, TILES)
        odd = lax.rem(sweep, 2)
        base = jnp.where(odd == 0, OFF - T + TILE * c, OFF + ROWS + T - TILE * (c + 1))
        sign = 2 * odd - 1

        @pl.when(it == 0)
        def _():
            raws[2].wait_recv()
            raws[3].wait_recv()
            diags[1].wait_recv()
            packs[0].wait_recv()

        @pl.when(it == 1)
        def _():
            packs[1].wait_recv()

        @pl.when(it == 2)
        def _():
            raws[0].wait_recv()
            raws[1].wait_recv()
            diags[0].wait_recv()
            packs[2].wait_recv()

        @pl.when(sweep == 0)
        def _():
            lax.fori_loop(c * (NG // UN), (c + 1) * (NG // UN), put, 0)

        prev = it - 1
        psweep, pc = lax.div(prev, TILES), lax.rem(prev, TILES)
        has_edge = (it > 0) & (pc != 1) & (psweep < SWEEPS - 1)
        pside = jnp.where(pc == 0, lax.rem(psweep, 2), 1 - lax.rem(psweep, 2))

        @pl.when(has_edge)
        def _():
            at = jnp.where(pside == 0, OFF, OFF + ROWS - T)
            for k in range(T // 8):
                q = pl.multiple_of(at + 8 * k, 8)
                for g in range(G):
                    sbuf[psweep, pside, 0, g, pl.ds(8 * k, 8), :] = st[0, g + 1, pl.ds(q, 8), :]
                    sbuf[psweep, pside, 1, g, pl.ds(8 * k, 8), :] = st[1, g + 1, pl.ds(q, 8), :]

        hside = jnp.where(c == 0, odd, 1 - odd)

        @pl.when((sweep > 0) & (c != 1))
        def _():
            exchange(sweep - 1, 1 - hside, down).wait_recv()
            at = jnp.where(hside == 0, OFF - T, OFF + ROWS)
            for k in range(T // 8):
                q = pl.multiple_of(at + 8 * k, 8)
                for g in range(G):
                    x = rbuf[sweep - 1, 1 - hside, 0, g, pl.ds(8 * k, 8), :]
                    st[0, g + 1, pl.ds(q, 8), :] = x
                    if g == 0:
                        st[0, G + 1, pl.ds(q, 8), :] = pltpu.roll(x, 127, 1)
                    if g == G - 1:
                        st[0, 0, pl.ds(q, 8), :] = pltpu.roll(x, 1, 1)
                    st[1, g + 1, pl.ds(q, 8), :] = rbuf[sweep - 1, 1 - hside, 1, g, pl.ds(8 * k, 8), :]

        def pair(i, _):
            t = sweep * T + 2 * i
            step(t, 0, base + sign * (2 * i + 1))
            step(t + 1, 1, base + sign * (2 * i + 2))

            @pl.when((i == 0) & has_edge)
            def _():
                exchange(psweep, pside, jnp.where(pside == 0, up, down)).start()

            return 0

        lax.fori_loop(0, T // 2, pair, 0)

        @pl.when(sweep == SWEEPS - 1)
        def _():
            lo = jnp.where(c == TILES - 1, 0, ROWS + 2 * T - TILE * (c + 1))
            hi = jnp.where(c == 0, ROWS, ROWS + 2 * T - TILE * c)
            lax.fori_loop(lax.div(lo, 8 * UN), lax.div(hi, 8 * UN), get_plain, 0)
            for k in range(TILES):
                @pl.when(c == k)
                def _():
                    for cp in out_copies(k):
                        cp.start()

        return 0

    lax.fori_loop(0, SWEEPS * TILES, tile, 0)

    for cp in raws + packs + diags:
        cp.wait_send()
    for e in range(SWEEPS - 1):
        for side in range(2):
            exchange(e, side, up).wait_send()
    for k in range(TILES):
        for cp in out_copies(k):
            cp.wait()


def solution(mesh):
    def local_run(u_tile, v_tile, w):
        dma = pltpu.SemaphoreType.DMA
        return pl.pallas_call(
            wave_kernel,
            out_shape=[jax.ShapeDtypeStruct((ROWS, COLS), F32)] * 2,
            in_specs=[pl.BlockSpec(memory_space=pl.ANY)] * 3,
            out_specs=[pl.BlockSpec(memory_space=pl.ANY)] * 2,
            scratch_shapes=[
                pltpu.VMEM((2, G + 2, R, 128), F32), pltpu.SMEM((3, 3, SWEEPS * T), F32), pltpu.VMEM((2 * G + 1, 8, 128), jnp.int32),
                pltpu.VMEM((ROWS + 2 * T, COLS), F32), pltpu.VMEM((ROWS + 2 * T, COLS), F32),
                pltpu.VMEM((2, ROWS, 128), F32), pltpu.VMEM((2, ROWS + 2 * T, 128), F32),
                pltpu.VMEM((ROWS, COLS), F32), pltpu.VMEM((ROWS, COLS), F32),
                pltpu.VMEM((SWEEPS - 1, 2, 2, G, T, 128), F32), pltpu.VMEM((SWEEPS - 1, 2, 2, G, T, 128), F32),
                dma((3,)), dma((2, 2)), dma((2, 2)), dma((TILES,)), dma((TILES,)), dma((2,)), dma((2,)),
                dma((SWEEPS - 1, 2)), dma((SWEEPS - 1, 2)), dma((2, TILES)),
            ],
            compiler_params=pltpu.CompilerParams(collective_id=0, has_side_effects=True),
        )(u_tile, v_tile, jnp.transpose(w, (1, 2, 0)))

    tile_spec = P(("ens", "row"), "col")
    return jax.shard_map(local_run, mesh=mesh, in_specs=(tile_spec, tile_spec, P()), out_specs=(tile_spec, tile_spec), check_vma=False)
```

time: 61 us -> 46 us (0.75)
  the two profiles are of different devices: /device:TPU:1 before, /device:TPU:0 now
where the time goes in v2:
time: 46 us; the launch traced here: 45.9 us
  Pallas kernels  42.5 us (92%)
  local copies, waits for them, and re-layouts  2.72 us (6%)
  between operations  0.65 us (1%)
    pallas_call x1, Pallas kernels, local_run(): pl.pallas_call(wave_kernel, out_shape=[jax.ShapeDtypeStruct((ROWS, COLS),...  42.5 us
    unnamed x4, local copies, waits for them, and re-layouts  2.72 us

profile of v2, /device:TPU:0, one launch (start us, length us, event | category | flops | bytes accessed | tf_op | source)
XLA Modules:
  0.0 45.9 jit_solution(11223617224789075754)
XLA Ops:
  0.6 42.5 %shard_map.50 = (f32[256,512]{1,0:T(8,128)}, f32[256,512]{1,0:T(8,128)}) custom-call(f32[256,512]{1,0:T(8,128)} %u_hbm.1, f32[256,512]{1,0:T(8,128)} %v_hbm.1, f32[3,3,64]{2,1,0:T(4,128)} %bitcast.1), custom_call_target="tpu_custom_call" | custom-call | tf_op jit(solution)/shard_map/pallas_call | solution.py:289
  43.1 0.0 copy-start
  43.2 1.9 %copy.7 = f32[256,512]{1,0:T(8,128)} copy(f32[256,512]{1,0:T(8,128)} %get-tuple-element.4) | data formatting | bytes 1048576
  45.1 0.0 copy-done
  45.1 0.8 %copy.8 = f32[256,512]{1,0:T(8,128)} copy(f32[256,512]{1,0:T(8,128)S(1)} %copy-done) | data formatting | bytes 1048576
Async XLA Ops:
  43.1 1.9 %copy-start = (f32[256,512]{1,0:T(8,128)S(1)}, f32[256,512]{1,0:T(8,128)}, u32[]{:S(2)}) copy-start(f32[256,512]{1,0:T(8,128)} %get-tuple-element.5) | copy-start | bytes 1572868

commit v3 on v2

--- a/solution.py
+++ b/solution.py
@@ -14,29 +14,46 @@
 TILES = 3
 TILE = (ROWS + 2 * T) // TILES
 NG = TILE // 8
+DROP = T // 8
 OFF = 40
 R = OFF + ROWS + OFF
-
-
-def wave_kernel(u_hbm, v_hbm, w_hbm, uo_hbm, vo_hbm, st, w_ref, maps, uraw, vraw, pbuf, hbuf, uout, vout, sbuf, rbuf,
-                load_sem, raw_ssem, raw_rsem, pk_ssem, pk_rsem, dg_ssem, dg_rsem, ex_ssem, ex_rsem, out_sem):
+VMEM_LIMIT = 55_300_000
+
+
+def wave_kernel(u_hbm, v_hbm, w_hbm, now_ref, before_ref, st, w_ref, maps, uraw, vraw, pbuf, hbuf, sbuf, rbuf,
+                load_sem, raw_ssem, raw_rsem, pk_ssem, pk_rsem, dg_ssem, dg_rsem, ex_ssem, ex_rsem):
     row = lax.axis_index("row")
     col = lax.axis_index("col")
     up = lax.rem(row + 3, 4)
     down = lax.rem(row + 1, 4)
     other = 1 - col
 
-    loads = [
-        pltpu.make_async_copy(u_hbm, uraw.at[pl.ds(T, ROWS)], load_sem.at[0]),
-        pltpu.make_async_copy(v_hbm, vraw.at[pl.ds(T, ROWS)], load_sem.at[1]),
-        pltpu.make_async_copy(w_hbm, w_ref, load_sem.at[2]),
-    ]
+    pieces = ((0, 128), (384, 128), (128, 256))
+    loads = [pltpu.make_async_copy(src.at[:, pl.ds(lo, n)], dst.at[pl.ds(T, ROWS), pl.ds(lo, n)], load_sem.at[f, k])
+             for k, (lo, n) in enumerate(pieces) for f, (src, dst) in enumerate(((u_hbm, uraw), (v_hbm, vraw)))]
+    loads.append(pltpu.make_async_copy(w_hbm, w_ref, load_sem.at[0, 3]))
     for cp in loads:
         cp.start()
 
     barrier = pltpu.get_barrier_semaphore()
     for rr, cc in ((row, other), (up, col), (down, col), (up, other), (down, other)):
         pl.semaphore_signal(barrier, inc=1, device_id={"row": rr, "col": cc}, device_id_type=MESH)
+    def zero(i, _):
+        for f in range(2):
+            for g in range(G + 2):
+                st[f, g, pl.ds(pl.multiple_of(i * 8, 8), 8), :] = jnp.zeros((8, 128), F32)
+        return 0
+
+    lax.fori_loop(0, (OFF - T) // 8, zero, 0)
+    lax.fori_loop((OFF + ROWS + T) // 8, R // 8, zero, 0)
+
+    lane = lax.broadcasted_iota(jnp.int32, (8, 128), 1)
+    maps[2 * G] = lax.rem(lane, G)
+    for g in range(G):
+        maps[g] = lax.rem(lane * G + (g + 64), 128)
+        k = lax.rem(3 * (lane + (2 * G - g - 1)), G)
+        maps[G + g] = lax.div(lax.rem(128 * k + lane + 64, 128 * G), G)
+
     pl.semaphore_wait(barrier, 5)
 
     def raw_copy(f, side):
@@ -71,23 +88,7 @@
     packs = [packed_copy(c) for c in range(TILES)]
     diags = [diag_copy(side) for side in range(2)]
 
-    def zero(i, _):
-        for f in range(2):
-            for g in range(G + 2):
-                st[f, g, pl.ds(pl.multiple_of(i * 8, 8), 8), :] = jnp.zeros((8, 128), F32)
-        return 0
-
-    lax.fori_loop(0, (OFF - T) // 8, zero, 0)
-    lax.fori_loop((OFF + ROWS + T) // 8, R // 8, zero, 0)
-
-    lane = lax.broadcasted_iota(jnp.int32, (8, 128), 1)
-    maps[2 * G] = lax.rem(lane, G)
-    for g in range(G):
-        maps[g] = lax.rem(lane * G + (g + 64), 128)
-        k = lax.rem(3 * (lane + (2 * G - g - 1)), G)
-        maps[G + g] = lax.div(lax.rem(128 * k + lane + 64, 128 * G), G)
-
-    for cp in loads:
+    for cp in loads[:4]:
         cp.wait()
 
     def pack(i, _):
@@ -104,6 +105,9 @@
     lax.fori_loop(cuts[1] // 8, (ROWS - T) // 8, pack, 0)
     packs[1].start()
     packs[2].start()
+
+    for cp in loads[4:]:
+        cp.wait()
 
     def lanes(x, idx):
         return jnp.take_along_axis(x, idx, axis=1, mode="promise_in_bounds")
@@ -133,12 +137,12 @@
                         st[0, 0, pl.ds(q, 8), :] = pltpu.roll(x, 1, 1)
         return 0
 
-    def step(t, src, start):
+    def step(t, src, start, ng):
         dst = 1 - src
         wa, wb, wc, wd, we = [0.5 * w_ref[a, b, t] for a, b in ((0, 0), (0, 1), (0, 2), (1, 0), (1, 1))]
         wa, wb, wc, wd, we = [jnp.full((8, 128), x, F32) for x in (wa, wb, wc, wd, 1.5 + we)]
-        sv = st.at[:, :, pl.ds(start - 1, TILE + 2)]
-        for i in range(NG):
+        sv = st.at[:, :, pl.ds(start - 1, 8 * ng + 2)]
+        for i in range(ng):
             n = [sv[src, g, pl.ds(8 * i, 8), :] for g in range(G + 2)]
             m = [sv[src, g, pl.ds(8 * i + 1, 8), :] for g in range(G + 2)]
             s = [sv[src, g, pl.ds(8 * i + 2, 8), :] for g in range(G + 2)]
@@ -159,13 +163,12 @@
 
     def get_plain(i, _):
         residue = maps[2 * G]
-        for f, out in ((0, uout), (1, vout)):
+        for f, out in ((0, now_ref), (1, before_ref)):
             zs = []
             for n in range(UN):
                 q = pl.multiple_of((i * UN + n) * 8 + OFF, 8)
                 for g in range(G):
-                    x = st[0, g + 1, pl.ds(q, 8), :]
-                    zs.append(4.0 * x if f == 0 else 8.0 * (x - st[1, g + 1, pl.ds(q, 8), :]))
+                    zs.append(st[f, g + 1, pl.ds(q, 8), :])
             for g in range(G):
                 idx = maps[G + g]
                 for n in range(UN):
@@ -178,13 +181,6 @@
                         x = jnp.where(residue == (g + 1 + 2 * k) % G, zs[n * G + g], x)
                     out[pl.ds(r, 8), 128 * k:128 * k + 128] = x
         return 0
-
-    ends = [ROWS] + [ROWS + T - TILE * (c + 1) + T for c in range(TILES - 1)] + [0]
-
-    def out_copies(c):
-        lo, n = ends[c + 1], ends[c] - ends[c + 1]
-        return [pltpu.make_async_copy(src.at[pl.ds(lo, n)], dst.at[pl.ds(lo, n)], out_sem.at[f, c])
-                for f, (src, dst) in enumerate(((uout, uo_hbm), (vout, vo_hbm)))]
 
     def tile(it, _):
         sweep, c = lax.div(it, TILES), lax.rem(it, TILES)
@@ -247,8 +243,8 @@
 
         def pair(i, _):
             t = sweep * T + 2 * i
-            step(t, 0, base + sign * (2 * i + 1))
-            step(t + 1, 1, base + sign * (2 * i + 2))
+            step(t, 0, base + sign * (2 * i + 1), NG)
+            step(t + 1, 1, base + sign * (2 * i + 2), NG)
 
             @pl.when((i == 0) & has_edge)
             def _():
@@ -256,18 +252,22 @@
 
             return 0
 
-        lax.fori_loop(0, T // 2, pair, 0)
+        def short_pair(i, _):
+            t = sweep * T + 2 * i
+            low = base + (1 - odd) * 8 * DROP
+            step(t, 0, low + sign * (2 * i + 1), NG - DROP)
+            step(t + 1, 1, low + sign * (2 * i + 2), NG - DROP)
+            return 0
+
+        half = jnp.where(c == 0, T // 4, T // 2)
+        lax.fori_loop(0, half, pair, 0)
+        lax.fori_loop(half, T // 2, short_pair, 0)
 
         @pl.when(sweep == SWEEPS - 1)
         def _():
             lo = jnp.where(c == TILES - 1, 0, ROWS + 2 * T - TILE * (c + 1))
             hi = jnp.where(c == 0, ROWS, ROWS + 2 * T - TILE * c)
             lax.fori_loop(lax.div(lo, 8 * UN), lax.div(hi, 8 * UN), get_plain, 0)
-            for k in range(TILES):
-                @pl.when(c == k)
-                def _():
-                    for cp in out_copies(k):
-                        cp.start()
 
         return 0
 
@@ -278,30 +278,27 @@
     for e in range(SWEEPS - 1):
         for side in range(2):
             exchange(e, side, up).wait_send()
-    for k in range(TILES):
-        for cp in out_copies(k):
-            cp.wait()
 
 
 def solution(mesh):
     def local_run(u_tile, v_tile, w):
         dma = pltpu.SemaphoreType.DMA
-        return pl.pallas_call(
+        now, before = pl.pallas_call(
             wave_kernel,
             out_shape=[jax.ShapeDtypeStruct((ROWS, COLS), F32)] * 2,
             in_specs=[pl.BlockSpec(memory_space=pl.ANY)] * 3,
-            out_specs=[pl.BlockSpec(memory_space=pl.ANY)] * 2,
+            out_specs=[pl.BlockSpec(memory_space=pltpu.VMEM)] * 2,
             scratch_shapes=[
                 pltpu.VMEM((2, G + 2, R, 128), F32), pltpu.SMEM((3, 3, SWEEPS * T), F32), pltpu.VMEM((2 * G + 1, 8, 128), jnp.int32),
                 pltpu.VMEM((ROWS + 2 * T, COLS), F32), pltpu.VMEM((ROWS + 2 * T, COLS), F32),
                 pltpu.VMEM((2, ROWS, 128), F32), pltpu.VMEM((2, ROWS + 2 * T, 128), F32),
-                pltpu.VMEM((ROWS, COLS), F32), pltpu.VMEM((ROWS, COLS), F32),
                 pltpu.VMEM((SWEEPS - 1, 2, 2, G, T, 128), F32), pltpu.VMEM((SWEEPS - 1, 2, 2, G, T, 128), F32),
-                dma((3,)), dma((2, 2)), dma((2, 2)), dma((TILES,)), dma((TILES,)), dma((2,)), dma((2,)),
-                dma((SWEEPS - 1, 2)), dma((SWEEPS - 1, 2)), dma((2, TILES)),
+                dma((2, 4)), dma((2, 2)), dma((2, 2)), dma((TILES,)), dma((TILES,)), dma((2,)), dma((2,)),
+                dma((SWEEPS - 1, 2)), dma((SWEEPS - 1, 2)),
             ],
-            compiler_params=pltpu.CompilerParams(collective_id=0, has_side_effects=True),
+            compiler_params=pltpu.CompilerParams(collective_id=0, has_side_effects=True, vmem_limit_bytes=VMEM_LIMIT),
         )(u_tile, v_tile, jnp.transpose(w, (1, 2, 0)))
+        return 4.0 * now, 8.0 * (now - before)
 
     tile_spec = P(("ens", "row"), "col")
     return jax.shard_map(local_run, mesh=mesh, in_specs=(tile_spec, tile_spec, P()), out_specs=(tile_spec, tile_spec), check_vma=False)

time: 46 us -> 43.8 us (0.952)
  local copies, waits for them, and re-layouts: 2.72 us -> 0.68 us
  Pallas kernels: 42.5 us -> 41.3 us
  other arithmetic: 0 us -> 1.09 us
    unnamed x4 -> x2, local copies, waits for them, and re-layouts: 2.72 us -> 0.68 us
    pallas_call x1, Pallas kernels: 42.5 us -> 41.3 us  [local_run(): pl.pallas_call(wave_kernel, out_shape=[jax.ShapeDtypeStruct((ROWS, COLS),...]
    mul x0 -> x1, other arithmetic: none -> 1.09 us  [local_run(): return (4.0 * now, 8.0 * (now - before))]
where the time goes in v3:
time: 43.8 us; the launch traced here: 43.7 us
  Pallas kernels  41.3 us (94%)
  other arithmetic  1.09 us (2%)
  local copies, waits for them, and re-layouts  0.68 us (2%)
  between operations  0.65 us (1%)
    pallas_call x1, Pallas kernels, local_run(): pl.pallas_call(wave_kernel, out_shape=[jax.ShapeDtypeStruct((ROWS, COLS),...  41.3 us
    mul x1, other arithmetic, local_run(): return (4.0 * now, 8.0 * (now - before))  1.09 us

profile of v3, /device:TPU:0, one launch (start us, length us, event | category | flops | bytes accessed | tf_op | source)
XLA Modules:
  0.0 43.7 jit_solution(1861867127484643534)
XLA Ops:
  0.6 0.0 copy-start
  0.6 0.7 %copy-done = f32[64,3,3]{0,2,1:T(4,128)S(1)} copy-done((f32[64,3,3]{0,2,1:T(4,128)S(1)}, f32[64,3,3]{0,2,1:T(4,128)}, u32[]{:S(2)}) %copy-start) | copy-done | bytes 2328
  1.3 41.3 %shard_map.50 = (f32[256,512]{1,0:T(8,128)S(1)}, f32[256,512]{1,0:T(8,128)S(1)}) custom-call(f32[256,512]{1,0:T(8,128)} %u_hbm.1, f32[256,512]{1,0:T(8,128)} %v_hbm.1, f32[3,3,64]{2,1,0:T(4,128)S(1)} %bitcast.1), custom_call_target="tpu_custom_call" | custom-call | tf_op jit(solution)/shard_map/pallas_call | solution.py:286
  42.6 1.1 %subtract_multiply_fusion = (f32[256,512]{1,0:T(8,128)}, f32[256,512]{1,0:T(8,128)}) fusion(f32[256,512]{1,0:T(8,128)S(1)} %get-tuple-element.4, f32[256,512]{1,0:T(8,128)S(1)} %get-tuple-element.5), kind=kLoop, calls=%fused_computation | loop fusion | flops 393216 | bytes 2097152 | tf_op jit(solution)/shard_map/mul | solution.py:301
Async XLA Ops:
  0.6 0.7 %copy-start = (f32[64,3,3]{0,2,1:T(4,128)S(1)}, f32[64,3,3]{0,2,1:T(4,128)}, u32[]{:S(2)}) copy-start(f32[64,3,3]{0,2,1:T(4,128)} %param.5) | copy-start | bytes 6916

commit v4 on v3

--- a/solution.py
+++ b/solution.py
@@ -15,6 +15,8 @@
 TILE = (ROWS + 2 * T) // TILES
 NG = TILE // 8
 DROP = T // 8
+RUN = 4
+BLOCK = 2
 OFF = 40
 R = OFF + ROWS + OFF
 VMEM_LIMIT = 55_300_000
@@ -137,23 +139,23 @@
                         st[0, 0, pl.ds(q, 8), :] = pltpu.roll(x, 1, 1)
         return 0
 
-    def step(t, src, start, ng):
-        dst = 1 - src
-        wa, wb, wc, wd, we = [0.5 * w_ref[a, b, t] for a, b in ((0, 0), (0, 1), (0, 2), (1, 0), (1, 1))]
-        wa, wb, wc, wd, we = [jnp.full((8, 128), x, F32) for x in (wa, wb, wc, wd, 1.5 + we)]
-        sv = st.at[:, :, pl.ds(start - 1, 8 * ng + 2)]
-        for i in range(ng):
-            n = [sv[src, g, pl.ds(8 * i, 8), :] for g in range(G + 2)]
-            m = [sv[src, g, pl.ds(8 * i + 1, 8), :] for g in range(G + 2)]
-            s = [sv[src, g, pl.ds(8 * i + 2, 8), :] for g in range(G + 2)]
-            for g in range(1, G + 1):
-                x = (wa * (n[g - 1] + s[g + 1]) + wc * (n[g + 1] + s[g - 1])) + (wb * (n[g] + s[g]) + wd * (m[g - 1] + m[g + 1]))
-                x = x + (we * m[g] - sv[dst, g, pl.ds(8 * i + 1, 8), :])
-                sv[dst, g, pl.ds(8 * i + 1, 8), :] = x
-                if g == 1:
-                    sv[dst, G + 1, pl.ds(8 * i + 1, 8), :] = pltpu.roll(x, 127, 1)
-                if g == G:
-                    sv[dst, 0, pl.ds(8 * i + 1, 8), :] = pltpu.roll(x, 1, 1)
+    def run(t, start, ng, sign):
+        low = min(0, sign * (RUN - 1))
+        sv = st.at[:, :, pl.ds(start + (low - 1), 8 * ng + RUN + 1)]
+        for k in range(RUN):
+            src, dst, at = k % 2, 1 - k % 2, 1 + sign * k - low
+            wa, wb, wc, wd, we = [0.5 * w_ref[a, b, t + k] for a, b in ((0, 0), (0, 1), (0, 2), (1, 0), (1, 1))]
+            wa, wb, wc, wd, we = [jnp.full((G, 8 * BLOCK, 128), x, F32) for x in (wa, wb, wc, wd, 1.5 + we)]
+            for i in range(0, ng, BLOCK):
+                q = at + 8 * i
+                n = sv[src, :, pl.ds(q - 1, 8 * BLOCK), :]
+                m = sv[src, :, pl.ds(q, 8 * BLOCK), :]
+                s = sv[src, :, pl.ds(q + 1, 8 * BLOCK), :]
+                x = (wa * (n[0:G] + s[2:G + 2]) + wc * (n[2:G + 2] + s[0:G])) + (wb * (n[1:G + 1] + s[1:G + 1]) + wd * (m[0:G] + m[2:G + 2]))
+                x = x + (we * m[1:G + 1] - sv[dst, 1:G + 1, pl.ds(q, 8 * BLOCK), :])
+                sv[dst, 1:G + 1, pl.ds(q, 8 * BLOCK), :] = x
+                sv[dst, G + 1, pl.ds(q, 8 * BLOCK), :] = pltpu.roll(x[0], 127, 1)
+                sv[dst, 0, pl.ds(q, 8 * BLOCK), :] = pltpu.roll(x[G - 1], 1, 1)
 
     def exchange(e, side, to):
         return pltpu.make_async_remote_copy(
@@ -186,7 +188,6 @@
         sweep, c = lax.div(it, TILES), lax.rem(it, TILES)
         odd = lax.rem(sweep, 2)
         base = jnp.where(odd == 0, OFF - T + TILE * c, OFF + ROWS + T - TILE * (c + 1))
-        sign = 2 * odd - 1
 
         @pl.when(it == 0)
         def _():
@@ -241,27 +242,32 @@
                         st[0, 0, pl.ds(q, 8), :] = pltpu.roll(x, 1, 1)
                     st[1, g + 1, pl.ds(q, 8), :] = rbuf[sweep - 1, 1 - hside, 1, g, pl.ds(8 * k, 8), :]
 
-        def pair(i, _):
-            t = sweep * T + 2 * i
-            step(t, 0, base + sign * (2 * i + 1), NG)
-            step(t + 1, 1, base + sign * (2 * i + 2), NG)
-
-            @pl.when((i == 0) & has_edge)
-            def _():
-                exchange(psweep, pside, jnp.where(pside == 0, up, down)).start()
-
-            return 0
-
-        def short_pair(i, _):
-            t = sweep * T + 2 * i
-            low = base + (1 - odd) * 8 * DROP
-            step(t, 0, low + sign * (2 * i + 1), NG - DROP)
-            step(t + 1, 1, low + sign * (2 * i + 2), NG - DROP)
-            return 0
-
-        half = jnp.where(c == 0, T // 4, T // 2)
-        lax.fori_loop(0, half, pair, 0)
-        lax.fori_loop(half, T // 2, short_pair, 0)
+        half = jnp.where(c == 0, T // (2 * RUN), T // RUN)
+
+        def steps(sign):
+            def full(i, _):
+                run(sweep * T + RUN * i, base + sign * (RUN * i + 1), NG, sign)
+
+                @pl.when((i == 0) & has_edge)
+                def _():
+                    exchange(psweep, pside, jnp.where(pside == 0, up, down)).start()
+
+                return 0
+
+            def short(i, _):
+                run(sweep * T + RUN * i, base + (8 * DROP if sign < 0 else 0) + sign * (RUN * i + 1), NG - DROP, sign)
+                return 0
+
+            lax.fori_loop(0, half, full, 0)
+            lax.fori_loop(half, T // RUN, short, 0)
+
+        @pl.when(odd == 0)
+        def _():
+            steps(-1)
+
+        @pl.when(odd == 1)
+        def _():
+            steps(1)
 
         @pl.when(sweep == SWEEPS - 1)
         def _():

time: 43.8 us -> 40.1 us (0.916)
  Pallas kernels: 41.3 us -> 37.5 us
    pallas_call x1, Pallas kernels: 41.3 us -> 37.5 us  [local_run(): pl.pallas_call(wave_kernel, out_shape=[jax.ShapeDtypeStruct((ROWS, COLS),...]
where the time goes in v4:
time: 40.1 us; the launch traced here: 39.9 us
  Pallas kernels  37.5 us (94%)
  other arithmetic  1.09 us (3%)
  local copies, waits for them, and re-layouts  0.68 us (2%)
  between operations  0.65 us (2%)
    pallas_call x1, Pallas kernels, local_run(): pl.pallas_call(wave_kernel, out_shape=[jax.ShapeDtypeStruct((ROWS, COLS),...  37.5 us
    mul x1, other arithmetic, local_run(): return (4.0 * now, 8.0 * (now - before))  1.09 us

profile of v4, /device:TPU:0, one launch (start us, length us, event | category | flops | bytes accessed | tf_op | source)
XLA Modules:
  0.0 39.9 jit_solution(15346920773388011214)
XLA Ops:
  0.6 0.0 copy-start
  0.6 0.7 %copy-done = f32[64,3,3]{0,2,1:T(4,128)S(1)} copy-done((f32[64,3,3]{0,2,1:T(4,128)S(1)}, f32[64,3,3]{0,2,1:T(4,128)}, u32[]{:S(2)}) %copy-start) | copy-done | bytes 2328
  1.3 37.5 %shard_map.50 = (f32[256,512]{1,0:T(8,128)S(1)}, f32[256,512]{1,0:T(8,128)S(1)}) custom-call(f32[256,512]{1,0:T(8,128)} %u_hbm.1, f32[256,512]{1,0:T(8,128)} %v_hbm.1, f32[3,3,64]{2,1,0:T(4,128)S(1)} %bitcast.1), custom_call_target="tpu_custom_call" | custom-call | tf_op jit(solution)/shard_map/pallas_call | solution.py:292
  38.8 1.1 %subtract_multiply_fusion = (f32[256,512]{1,0:T(8,128)}, f32[256,512]{1,0:T(8,128)}) fusion(f32[256,512]{1,0:T(8,128)S(1)} %get-tuple-element.4, f32[256,512]{1,0:T(8,128)S(1)} %get-tuple-element.5), kind=kLoop, calls=%fused_computation | loop fusion | flops 393216 | bytes 2097152 | tf_op jit(solution)/shard_map/mul | solution.py:307
Async XLA Ops:
  0.6 0.7 %copy-start = (f32[64,3,3]{0,2,1:T(4,128)S(1)}, f32[64,3,3]{0,2,1:T(4,128)}, u32[]{:S(2)}) copy-start(f32[64,3,3]{0,2,1:T(4,128)} %param.5) | copy-start | bytes 6916

commit v5 on v4

--- a/solution.py
+++ b/solution.py
@@ -15,10 +15,9 @@
 TILE = (ROWS + 2 * T) // TILES
 NG = TILE // 8
 DROP = T // 8
-RUN = 4
-BLOCK = 2
-OFF = 40
-R = OFF + ROWS + OFF
+RUN = 8
+OFF = 32
+R = 328
 VMEM_LIMIT = 55_300_000
 
 
@@ -141,47 +140,45 @@
 
     def run(t, start, ng, sign):
         low = min(0, sign * (RUN - 1))
+        rows = 32 if ng % 4 == 0 else 16
         sv = st.at[:, :, pl.ds(start + (low - 1), 8 * ng + RUN + 1)]
         for k in range(RUN):
             src, dst, at = k % 2, 1 - k % 2, 1 + sign * k - low
             wa, wb, wc, wd, we = [0.5 * w_ref[a, b, t + k] for a, b in ((0, 0), (0, 1), (0, 2), (1, 0), (1, 1))]
-            wa, wb, wc, wd, we = [jnp.full((G, 8 * BLOCK, 128), x, F32) for x in (wa, wb, wc, wd, 1.5 + we)]
-            for i in range(0, ng, BLOCK):
-                q = at + 8 * i
-                n = sv[src, :, pl.ds(q - 1, 8 * BLOCK), :]
-                m = sv[src, :, pl.ds(q, 8 * BLOCK), :]
-                s = sv[src, :, pl.ds(q + 1, 8 * BLOCK), :]
+            wa, wb, wc, wd, we = [jnp.full((G, rows, 128), x, F32) for x in (wa, wb, wc, wd, 1.5 + we)]
+            for q in range(at, at + 8 * ng, rows):
+                n = sv[src, :, pl.ds(q - 1, rows), :]
+                m = sv[src, :, pl.ds(q, rows), :]
+                s = sv[src, :, pl.ds(q + 1, rows), :]
                 x = (wa * (n[0:G] + s[2:G + 2]) + wc * (n[2:G + 2] + s[0:G])) + (wb * (n[1:G + 1] + s[1:G + 1]) + wd * (m[0:G] + m[2:G + 2]))
-                x = x + (we * m[1:G + 1] - sv[dst, 1:G + 1, pl.ds(q, 8 * BLOCK), :])
-                sv[dst, 1:G + 1, pl.ds(q, 8 * BLOCK), :] = x
-                sv[dst, G + 1, pl.ds(q, 8 * BLOCK), :] = pltpu.roll(x[0], 127, 1)
-                sv[dst, 0, pl.ds(q, 8 * BLOCK), :] = pltpu.roll(x[G - 1], 1, 1)
-
-    def exchange(e, side, to):
+                x = x + (we * m[1:G + 1] - sv[dst, 1:G + 1, pl.ds(q, rows), :])
+                sv[dst, 1:G + 1, pl.ds(q, rows), :] = x
+                sv[dst, G + 1, pl.ds(q, rows), :] = pltpu.roll(x[0], 127, 1)
+                sv[dst, 0, pl.ds(q, rows), :] = pltpu.roll(x[G - 1], 1, 1)
+
+    def exchange(e, side, to, late):
+        src = sbuf.at[e] if late else st.at[:, pl.ds(1, G), pl.ds(jnp.where(side == 0, OFF, OFF + ROWS - T), T)]
         return pltpu.make_async_remote_copy(
-            src_ref=sbuf.at[e, side], dst_ref=rbuf.at[e, side],
+            src_ref=src, dst_ref=rbuf.at[e, side],
             send_sem=ex_ssem.at[e, side], recv_sem=ex_rsem.at[e, side],
             device_id={"row": to, "col": col}, device_id_type=MESH)
 
     def get_plain(i, _):
         residue = maps[2 * G]
-        for f, out in ((0, now_ref), (1, before_ref)):
-            zs = []
-            for n in range(UN):
-                q = pl.multiple_of((i * UN + n) * 8 + OFF, 8)
-                for g in range(G):
-                    zs.append(st[f, g + 1, pl.ds(q, 8), :])
-            for g in range(G):
-                idx = maps[G + g]
-                for n in range(UN):
-                    zs[n * G + g] = lanes(zs[n * G + g], idx)
-            for n in range(UN):
-                r = pl.multiple_of((i * UN + n) * 8, 8)
-                for k in range(4):
-                    x = zs[n * G]
-                    for g in range(1, G):
-                        x = jnp.where(residue == (g + 1 + 2 * k) % G, zs[n * G + g], x)
-                    out[pl.ds(r, 8), 128 * k:128 * k + 128] = x
+        outs = [(f, n) for f in range(2) for n in range(2)]
+        zs = {}
+        for g in range(G):
+            idx = maps[G + g]
+            for f, n in outs:
+                q = pl.multiple_of((i * 2 + n) * 8 + OFF, 8)
+                zs[f, n, g] = lanes(st[f, g + 1, pl.ds(q, 8), :], idx)
+        for f, n in outs:
+            r = pl.multiple_of((i * 2 + n) * 8, 8)
+            for k in range(4):
+                x = zs[f, n, 0]
+                for g in range(1, G):
+                    x = jnp.where(residue == (g + 1 + 2 * k) % G, zs[f, n, g], x)
+                (now_ref, before_ref)[f][pl.ds(r, 8), 128 * k:128 * k + 128] = x
         return 0
 
     def tile(it, _):
@@ -211,47 +208,51 @@
         def _():
             lax.fori_loop(c * (NG // UN), (c + 1) * (NG // UN), put, 0)
 
-        prev = it - 1
-        psweep, pc = lax.div(prev, TILES), lax.rem(prev, TILES)
-        has_edge = (it > 0) & (pc != 1) & (psweep < SWEEPS - 1)
-        pside = jnp.where(pc == 0, lax.rem(psweep, 2), 1 - lax.rem(psweep, 2))
-
-        @pl.when(has_edge)
-        def _():
-            at = jnp.where(pside == 0, OFF, OFF + ROWS - T)
+        first = odd
+        last = 1 - odd
+        to_first = jnp.where(odd == 0, up, down)
+        to_last = jnp.where(odd == 0, down, up)
+
+        def put_rows(side):
+            at = jnp.where(side == 0, OFF - T, OFF + ROWS)
             for k in range(T // 8):
                 q = pl.multiple_of(at + 8 * k, 8)
                 for g in range(G):
-                    sbuf[psweep, pside, 0, g, pl.ds(8 * k, 8), :] = st[0, g + 1, pl.ds(q, 8), :]
-                    sbuf[psweep, pside, 1, g, pl.ds(8 * k, 8), :] = st[1, g + 1, pl.ds(q, 8), :]
-
-        hside = jnp.where(c == 0, odd, 1 - odd)
-
-        @pl.when((sweep > 0) & (c != 1))
-        def _():
-            exchange(sweep - 1, 1 - hside, down).wait_recv()
-            at = jnp.where(hside == 0, OFF - T, OFF + ROWS)
-            for k in range(T // 8):
-                q = pl.multiple_of(at + 8 * k, 8)
-                for g in range(G):
-                    x = rbuf[sweep - 1, 1 - hside, 0, g, pl.ds(8 * k, 8), :]
+                    x = rbuf[sweep - 1, 1 - side, 0, g, pl.ds(8 * k, 8), :]
                     st[0, g + 1, pl.ds(q, 8), :] = x
                     if g == 0:
                         st[0, G + 1, pl.ds(q, 8), :] = pltpu.roll(x, 127, 1)
                     if g == G - 1:
                         st[0, 0, pl.ds(q, 8), :] = pltpu.roll(x, 1, 1)
-                    st[1, g + 1, pl.ds(q, 8), :] = rbuf[sweep - 1, 1 - hside, 1, g, pl.ds(8 * k, 8), :]
+                    st[1, g + 1, pl.ds(q, 8), :] = rbuf[sweep - 1, 1 - side, 1, g, pl.ds(8 * k, 8), :]
+
+        @pl.when((sweep > 0) & (c == 0))
+        def _():
+            at = jnp.where(first == 0, OFF, OFF + ROWS - T)
+            for k in range(T // 8):
+                q = pl.multiple_of(at + 8 * k, 8)
+                for f in range(2):
+                    for g in range(G):
+                        sbuf[sweep - 1, f, g, pl.ds(8 * k, 8), :] = st[f, g + 1, pl.ds(q, 8), :]
+            exchange(sweep - 1, 1 - first, up, True).wait_recv()
+            put_rows(first)
+            exchange(sweep - 1, first, to_first, True).start()
+
+        @pl.when((sweep < SWEEPS - 1) & (c == 1))
+        def _():
+            exchange(sweep, first, to_first, False).start()
+
+        @pl.when((sweep > 0) & (c == TILES - 1))
+        def _():
+            exchange(sweep - 1, last, up, False).wait_send()
+            exchange(sweep - 1, 1 - last, up, True).wait_recv()
+            put_rows(last)
 
         half = jnp.where(c == 0, T // (2 * RUN), T // RUN)
 
         def steps(sign):
             def full(i, _):
                 run(sweep * T + RUN * i, base + sign * (RUN * i + 1), NG, sign)
-
-                @pl.when((i == 0) & has_edge)
-                def _():
-                    exchange(psweep, pside, jnp.where(pside == 0, up, down)).start()
-
                 return 0
 
             def short(i, _):
@@ -273,7 +274,7 @@
         def _():
             lo = jnp.where(c == TILES - 1, 0, ROWS + 2 * T - TILE * (c + 1))
             hi = jnp.where(c == 0, ROWS, ROWS + 2 * T - TILE * c)
-            lax.fori_loop(lax.div(lo, 8 * UN), lax.div(hi, 8 * UN), get_plain, 0)
+            lax.fori_loop(lax.div(lo, 16), lax.div(hi, 16), get_plain, 0)
 
         return 0
 
@@ -282,8 +283,7 @@
     for cp in raws + packs + diags:
         cp.wait_send()
     for e in range(SWEEPS - 1):
-        for side in range(2):
-            exchange(e, side, up).wait_send()
+        exchange(e, (e + 1) % 2, up, True).wait_send()
 
 
 def solution(mesh):
@@ -298,7 +298,7 @@
                 pltpu.VMEM((2, G + 2, R, 128), F32), pltpu.SMEM((3, 3, SWEEPS * T), F32), pltpu.VMEM((2 * G + 1, 8, 128), jnp.int32),
                 pltpu.VMEM((ROWS + 2 * T, COLS), F32), pltpu.VMEM((ROWS + 2 * T, COLS), F32),
                 pltpu.VMEM((2, ROWS, 128), F32), pltpu.VMEM((2, ROWS + 2 * T, 128), F32),
-                pltpu.VMEM((SWEEPS - 1, 2, 2, G, T, 128), F32), pltpu.VMEM((SWEEPS - 1, 2, 2, G, T, 128), F32),
+                pltpu.VMEM((SWEEPS - 1, 2, G, T, 128), F32), pltpu.VMEM((SWEEPS - 1, 2, 2, G, T, 128), F32),
                 dma((2, 4)), dma((2, 2)), dma((2, 2)), dma((TILES,)), dma((TILES,)), dma((2,)), dma((2,)),
                 dma((SWEEPS - 1, 2)), dma((SWEEPS - 1, 2)),
             ],

time: 40.1 us -> 39.3 us (0.980)
  Pallas kernels: 37.5 us -> 36.8 us
    pallas_call x1, Pallas kernels: 37.5 us -> 36.8 us  [local_run(): pl.pallas_call(wave_kernel, out_shape=[jax.ShapeDtypeStruct((ROWS, COLS),...]
where the time goes in v5:
time: 39.3 us; the launch traced here: 39.2 us
  Pallas kernels  36.8 us (94%)
  other arithmetic  1.09 us (3%)
  local copies, waits for them, and re-layouts  0.68 us (2%)
  between operations  0.65 us (2%)
    pallas_call x1, Pallas kernels, local_run(): pl.pallas_call(wave_kernel, out_shape=[jax.ShapeDtypeStruct((ROWS, COLS),...  36.8 us
    mul x1, other arithmetic, local_run(): return (4.0 * now, 8.0 * (now - before))  1.09 us

profile of v5, /device:TPU:0, one launch (start us, length us, event | category | flops | bytes accessed | tf_op | source)
XLA Modules:
  0.0 39.2 jit_solution(15958488768000702889)
XLA Ops:
  0.6 0.0 copy-start
  0.6 0.7 %copy-done = f32[64,3,3]{0,2,1:T(4,128)S(1)} copy-done((f32[64,3,3]{0,2,1:T(4,128)S(1)}, f32[64,3,3]{0,2,1:T(4,128)}, u32[]{:S(2)}) %copy-start) | copy-done | bytes 2328
  1.3 36.8 %shard_map.50 = (f32[256,512]{1,0:T(8,128)S(1)}, f32[256,512]{1,0:T(8,128)S(1)}) custom-call(f32[256,512]{1,0:T(8,128)} %u_hbm.1, f32[256,512]{1,0:T(8,128)} %v_hbm.1, f32[3,3,64]{2,1,0:T(4,128)S(1)} %bitcast.1), custom_call_target="tpu_custom_call" | custom-call | tf_op jit(solution)/shard_map/pallas_call | solution.py:292
  38.1 1.1 %subtract_multiply_fusion = (f32[256,512]{1,0:T(8,128)}, f32[256,512]{1,0:T(8,128)}) fusion(f32[256,512]{1,0:T(8,128)S(1)} %get-tuple-element.4, f32[256,512]{1,0:T(8,128)S(1)} %get-tuple-element.5), kind=kLoop, calls=%fused_computation | loop fusion | flops 393216 | bytes 2097152 | tf_op jit(solution)/shard_map/mul | solution.py:307
Async XLA Ops:
  0.6 0.7 %copy-start = (f32[64,3,3]{0,2,1:T(4,128)S(1)}, f32[64,3,3]{0,2,1:T(4,128)}, u32[]{:S(2)}) copy-start(f32[64,3,3]{0,2,1:T(4,128)} %param.5) | copy-start | bytes 6916

commit v6 on v5

--- a/solution.py
+++ b/solution.py
@@ -21,7 +21,7 @@
 VMEM_LIMIT = 55_300_000
 
 
-def wave_kernel(u_hbm, v_hbm, w_hbm, now_ref, before_ref, st, w_ref, maps, uraw, vraw, pbuf, hbuf, sbuf, rbuf,
+def wave_kernel(u_hbm, v_hbm, w_hbm, now_ref, before_ref, st, w_ref, maps, uraw, vraw, pbuf, hbuf, zbuf, sbuf, rbuf,
                 load_sem, raw_ssem, raw_rsem, pk_ssem, pk_rsem, dg_ssem, dg_rsem, ex_ssem, ex_rsem):
     row = lax.axis_index("row")
     col = lax.axis_index("col")
@@ -113,34 +113,29 @@
     def lanes(x, idx):
         return jnp.take_along_axis(x, idx, axis=1, mode="promise_in_bounds")
 
-    UN = 4
-
-    def put(i, _):
+    def put(c):
         residue = maps[2 * G]
-        rows = [(pl.multiple_of((i * UN + n) * 8, 8), pl.multiple_of((i * UN + n) * 8 + (OFF - T), 8)) for n in range(UN)]
-        srcs = []
-        for r, q in rows:
-            us = [0.25 * uraw[pl.ds(r, 8), 128 * k:128 * k + 128] for k in range(4)] + [0.25 * hbuf[0, pl.ds(r, 8), :]]
-            vs = [vraw[pl.ds(r, 8), 128 * k:128 * k + 128] for k in range(4)] + [hbuf[1, pl.ds(r, 8), :]]
-            srcs.append((us, [u - 0.125 * v for u, v in zip(us, vs)]))
         for g in range(G):
             idx = maps[g]
-            for (r, q), pair in zip(rows, srcs):
-                for f in range(2):
-                    x = pair[f][4]
-                    for k in range(4):
-                        x = jnp.where(residue == (g + 1 + 2 * k) % G, pair[f][k], x)
-                    x = lanes(x, idx)
-                    st[f, g + 1, pl.ds(q, 8), :] = x
-                    if f == 0 and g == 0:
-                        st[0, G + 1, pl.ds(q, 8), :] = pltpu.roll(x, 127, 1)
-                    if f == 0 and g == G - 1:
-                        st[0, 0, pl.ds(q, 8), :] = pltpu.roll(x, 1, 1)
-        return 0
+            for n in range(NG):
+                r = pl.multiple_of(c * TILE + 8 * n, 8)
+                q = pl.multiple_of(c * TILE + (OFF - T + 8 * n), 8)
+                u, v = hbuf[0, pl.ds(r, 8), :], hbuf[1, pl.ds(r, 8), :]
+                for k in range(4):
+                    mask = residue == (g + 1 + 2 * k) % G
+                    u = jnp.where(mask, uraw[pl.ds(r, 8), 128 * k:128 * k + 128], u)
+                    v = jnp.where(mask, vraw[pl.ds(r, 8), 128 * k:128 * k + 128], v)
+                x = 0.25 * lanes(u, idx)
+                st[0, g + 1, pl.ds(q, 8), :] = x
+                st[1, g + 1, pl.ds(q, 8), :] = x - 0.125 * lanes(v, idx)
+        for n in range(NG):
+            q = pl.multiple_of(c * TILE + (OFF - T + 8 * n), 8)
+            st[0, G + 1, pl.ds(q, 8), :] = pltpu.roll(st[0, 1, pl.ds(q, 8), :], 127, 1)
+            st[0, 0, pl.ds(q, 8), :] = pltpu.roll(st[0, G, pl.ds(q, 8), :], 1, 1)
 
     def run(t, start, ng, sign):
         low = min(0, sign * (RUN - 1))
-        rows = 32 if ng % 4 == 0 else 16
+        rows = 16
         sv = st.at[:, :, pl.ds(start + (low - 1), 8 * ng + RUN + 1)]
         for k in range(RUN):
             src, dst, at = k % 2, 1 - k % 2, 1 + sign * k - low
@@ -163,23 +158,22 @@
             send_sem=ex_ssem.at[e, side], recv_sem=ex_rsem.at[e, side],
             device_id={"row": to, "col": col}, device_id_type=MESH)
 
-    def get_plain(i, _):
-        residue = maps[2 * G]
-        outs = [(f, n) for f in range(2) for n in range(2)]
-        zs = {}
+    def get(lo):
         for g in range(G):
             idx = maps[G + g]
-            for f, n in outs:
-                q = pl.multiple_of((i * 2 + n) * 8 + OFF, 8)
-                zs[f, n, g] = lanes(st[f, g + 1, pl.ds(q, 8), :], idx)
-        for f, n in outs:
-            r = pl.multiple_of((i * 2 + n) * 8, 8)
-            for k in range(4):
-                x = zs[f, n, 0]
-                for g in range(1, G):
-                    x = jnp.where(residue == (g + 1 + 2 * k) % G, zs[f, n, g], x)
-                (now_ref, before_ref)[f][pl.ds(r, 8), 128 * k:128 * k + 128] = x
-        return 0
+            for n in range(NG):
+                q = pl.multiple_of(lo + (OFF + 8 * n), 8)
+                for f in range(2):
+                    zbuf[f, g, 8 * n:8 * n + 8, :] = lanes(st[f, g + 1, pl.ds(q, 8), :], idx)
+        residue = maps[2 * G]
+        for n in range(NG):
+            r = pl.multiple_of(lo + 8 * n, 8)
+            for f, out in ((0, now_ref), (1, before_ref)):
+                for k in range(4):
+                    x = zbuf[f, 0, 8 * n:8 * n + 8, :]
+                    for g in range(1, G):
+                        x = jnp.where(residue == (g + 1 + 2 * k) % G, zbuf[f, g, 8 * n:8 * n + 8, :], x)
+                    out[pl.ds(r, 8), 128 * k:128 * k + 128] = x
 
     def tile(it, _):
         sweep, c = lax.div(it, TILES), lax.rem(it, TILES)
@@ -206,7 +200,7 @@
 
         @pl.when(sweep == 0)
         def _():
-            lax.fori_loop(c * (NG // UN), (c + 1) * (NG // UN), put, 0)
+            put(c)
 
         first = odd
         last = 1 - odd
@@ -272,9 +266,7 @@
 
         @pl.when(sweep == SWEEPS - 1)
         def _():
-            lo = jnp.where(c == TILES - 1, 0, ROWS + 2 * T - TILE * (c + 1))
-            hi = jnp.where(c == 0, ROWS, ROWS + 2 * T - TILE * c)
-            lax.fori_loop(lax.div(lo, 16), lax.div(hi, 16), get_plain, 0)
+            get(pl.multiple_of(jnp.where(c == 0, ROWS - TILE, (TILES - 1 - c) * TILE), 8))
 
         return 0
 
@@ -297,13 +289,13 @@
             scratch_shapes=[
                 pltpu.VMEM((2, G + 2, R, 128), F32), pltpu.SMEM((3, 3, SWEEPS * T), F32), pltpu.VMEM((2 * G + 1, 8, 128), jnp.int32),
                 pltpu.VMEM((ROWS + 2 * T, COLS), F32), pltpu.VMEM((ROWS + 2 * T, COLS), F32),
-                pltpu.VMEM((2, ROWS, 128), F32), pltpu.VMEM((2, ROWS + 2 * T, 128), F32),
+                pltpu.VMEM((2, ROWS, 128), F32), pltpu.VMEM((2, ROWS + 2 * T, 128), F32), pltpu.VMEM((2, G, TILE, 128), F32),
                 pltpu.VMEM((SWEEPS - 1, 2, G, T, 128), F32), pltpu.VMEM((SWEEPS - 1, 2, 2, G, T, 128), F32),
                 dma((2, 4)), dma((2, 2)), dma((2, 2)), dma((TILES,)), dma((TILES,)), dma((2,)), dma((2,)),
                 dma((SWEEPS - 1, 2)), dma((SWEEPS - 1, 2)),
             ],
             compiler_params=pltpu.CompilerParams(collective_id=0, has_side_effects=True, vmem_limit_bytes=VMEM_LIMIT),
-        )(u_tile, v_tile, jnp.transpose(w, (1, 2, 0)))
+        )(u_tile, v_tile, pltpu.with_memory_space_constraint(jnp.transpose(w, (1, 2, 0)), pltpu.HBM))
         return 4.0 * now, 8.0 * (now - before)
 
     tile_spec = P(("ens", "row"), "col")

time: 39.3 us -> 36.4 us (0.926)
  Pallas kernels: 36.8 us -> 34.6 us
  local copies, waits for them, and re-layouts: 0.68 us -> 0 us
    pallas_call x1, Pallas kernels: 36.8 us -> 34.6 us  [local_run(): pl.pallas_call(wave_kernel, out_shape=[jax.ShapeDtypeStruct((ROWS, COLS),...]
    unnamed x2 -> x0, local copies, waits for them, and re-layouts: 0.68 us -> none
where the time goes in v6:
time: 36.4 us; the launch traced here: 36.3 us
  Pallas kernels  34.6 us (95%)
  other arithmetic  1.08 us (3%)
  between operations  0.64 us (2%)
    pallas_call x1, Pallas kernels, local_run(): pl.pallas_call(wave_kernel, out_shape=[jax.ShapeDtypeStruct((ROWS, COLS),...  34.6 us
    mul x1, other arithmetic, local_run(): return (4.0 * now, 8.0 * (now - before))  1.08 us

profile of v6, /device:TPU:0, one launch (start us, length us, event | category | flops | bytes accessed | tf_op | source)
XLA Modules:
  0.0 36.3 jit_solution(724558978980580382)
XLA Ops:
  0.6 34.6 %shard_map.50 = (f32[256,512]{1,0:T(8,128)S(1)}, f32[256,512]{1,0:T(8,128)S(1)}) custom-call(f32[256,512]{1,0:T(8,128)} %u_hbm.1, f32[256,512]{1,0:T(8,128)} %v_hbm.1, f32[3,3,64]{2,1,0:T(4,128)} %bitcast.1), custom_call_target="tpu_custom_call" | custom-call | tf_op jit(solution)/shard_map/pallas_call | solution.py:284
  35.2 1.1 %subtract_multiply_fusion = (f32[256,512]{1,0:T(8,128)}, f32[256,512]{1,0:T(8,128)}) fusion(f32[256,512]{1,0:T(8,128)S(1)} %get-tuple-element.4, f32[256,512]{1,0:T(8,128)S(1)} %get-tuple-element.5), kind=kLoop, calls=%fused_computation | loop fusion | flops 393216 | bytes 2097152 | tf_op jit(solution)/shard_map/mul | solution.py:299

commit v7 on v6

--- a/solution.py
+++ b/solution.py
@@ -14,8 +14,7 @@
 TILES = 3
 TILE = (ROWS + 2 * T) // TILES
 NG = TILE // 8
-DROP = T // 8
-RUN = 8
+BLOCK = 4
 OFF = 32
 R = 328
 VMEM_LIMIT = 55_300_000
@@ -29,16 +28,20 @@
     down = lax.rem(row + 1, 4)
     other = 1 - col
 
-    pieces = ((0, 128), (384, 128), (128, 256))
-    loads = [pltpu.make_async_copy(src.at[:, pl.ds(lo, n)], dst.at[pl.ds(T, ROWS), pl.ds(lo, n)], load_sem.at[f, k])
-             for k, (lo, n) in enumerate(pieces) for f, (src, dst) in enumerate(((u_hbm, uraw), (v_hbm, vraw)))]
-    loads.append(pltpu.make_async_copy(w_hbm, w_ref, load_sem.at[0, 3]))
-    for cp in loads:
-        cp.start()
-
     barrier = pltpu.get_barrier_semaphore()
     for rr, cc in ((row, other), (up, col), (down, col), (up, other), (down, other)):
         pl.semaphore_signal(barrier, inc=1, device_id={"row": rr, "col": cc}, device_id_type=MESH)
+
+    cuts = [0] + [TILE * (c + 1) - T for c in range(TILES - 1)] + [ROWS]
+
+    pieces = [(lo, n, at, 128) for lo, n in ((ROWS - T, T), (0, cuts[1]), (cuts[1], ROWS - T - cuts[1])) for at in (0, COLS - 128)]
+    pieces.append((0, ROWS, 128, COLS - 256))
+    loads = [pltpu.make_async_copy(src.at[pl.ds(lo, n), pl.ds(at, m)], dst.at[pl.ds(T + lo, n), pl.ds(at, m)], load_sem.at[f, k])
+             for k, (lo, n, at, m) in enumerate(pieces) for f, (src, dst) in enumerate(((u_hbm, uraw), (v_hbm, vraw)))]
+    loads.append(pltpu.make_async_copy(w_hbm, w_ref, load_sem.at[0, len(pieces)]))
+    for cp in loads:
+        cp.start()
+
     def zero(i, _):
         for f in range(2):
             for g in range(G + 2):
@@ -70,8 +73,6 @@
     for cp in raws[2:] + raws[:2]:
         cp.start()
 
-    cuts = [0] + [TILE * (c + 1) - T for c in range(TILES - 1)] + [ROWS]
-
     def packed_copy(c):
         n = cuts[c + 1] - cuts[c]
         return pltpu.make_async_remote_copy(
@@ -89,7 +90,7 @@
     packs = [packed_copy(c) for c in range(TILES)]
     diags = [diag_copy(side) for side in range(2)]
 
-    for cp in loads[:4]:
+    for cp in loads[:8]:
         cp.wait()
 
     def pack(i, _):
@@ -103,11 +104,13 @@
     diags[1].start()
     packs[0].start()
     diags[0].start()
+    for cp in loads[8:12]:
+        cp.wait()
     lax.fori_loop(cuts[1] // 8, (ROWS - T) // 8, pack, 0)
     packs[1].start()
     packs[2].start()
 
-    for cp in loads[4:]:
+    for cp in loads[12:]:
         cp.wait()
 
     def lanes(x, idx):
@@ -133,20 +136,28 @@
             st[0, G + 1, pl.ds(q, 8), :] = pltpu.roll(st[0, 1, pl.ds(q, 8), :], 127, 1)
             st[0, 0, pl.ds(q, 8), :] = pltpu.roll(st[0, G, pl.ds(q, 8), :], 1, 1)
 
-    def run(t, start, ng, sign):
-        low = min(0, sign * (RUN - 1))
-        rows = 16
-        sv = st.at[:, :, pl.ds(start + (low - 1), 8 * ng + RUN + 1)]
-        for k in range(RUN):
-            src, dst, at = k % 2, 1 - k % 2, 1 + sign * k - low
+    def run(t, base, sign, first):
+        drops = [2 * (k + 1) // 8 if first else 0 for k in range(T)]
+        tops = [sign * (k + 1) + (8 * drops[k] if sign < 0 else 0) for k in range(T)]
+        low = min(tops) - 1
+        high = max(top + TILE - 8 * drop for top, drop in zip(tops, drops)) + 1
+        sv = st.at[:, :, pl.ds(base + low, high - low)]
+        for k in range(T):
+            src, dst = k % 2, 1 - k % 2
             wa, wb, wc, wd, we = [0.5 * w_ref[a, b, t + k] for a, b in ((0, 0), (0, 1), (0, 2), (1, 0), (1, 1))]
-            wa, wb, wc, wd, we = [jnp.full((G, rows, 128), x, F32) for x in (wa, wb, wc, wd, 1.5 + we)]
-            for q in range(at, at + 8 * ng, rows):
+            blocks = []
+            at, left = tops[k] - low, NG - drops[k]
+            while left:
+                n = min(left, BLOCK if left > BLOCK + 1 or left == BLOCK else (left + 1) // 2)
+                blocks.append((at, 8 * n))
+                at, left = at + 8 * n, left - n
+            for q, rows in blocks if sign < 0 else blocks[::-1]:
+                ca, cb, cc, cd, ce = [jnp.full((G, rows, 128), x, F32) for x in (wa, wb, wc, wd, 1.5 + we)]
                 n = sv[src, :, pl.ds(q - 1, rows), :]
                 m = sv[src, :, pl.ds(q, rows), :]
                 s = sv[src, :, pl.ds(q + 1, rows), :]
-                x = (wa * (n[0:G] + s[2:G + 2]) + wc * (n[2:G + 2] + s[0:G])) + (wb * (n[1:G + 1] + s[1:G + 1]) + wd * (m[0:G] + m[2:G + 2]))
-                x = x + (we * m[1:G + 1] - sv[dst, 1:G + 1, pl.ds(q, rows), :])
+                x = (ca * (n[0:G] + s[2:G + 2]) + cc * (n[2:G + 2] + s[0:G])) + (cb * (n[1:G + 1] + s[1:G + 1]) + cd * (m[0:G] + m[2:G + 2]))
+                x = x + (ce * m[1:G + 1] - sv[dst, 1:G + 1, pl.ds(q, rows), :])
                 sv[dst, 1:G + 1, pl.ds(q, rows), :] = x
                 sv[dst, G + 1, pl.ds(q, rows), :] = pltpu.roll(x[0], 127, 1)
                 sv[dst, 0, pl.ds(q, rows), :] = pltpu.roll(x[G - 1], 1, 1)
@@ -242,27 +253,11 @@
             exchange(sweep - 1, 1 - last, up, True).wait_recv()
             put_rows(last)
 
-        half = jnp.where(c == 0, T // (2 * RUN), T // RUN)
-
-        def steps(sign):
-            def full(i, _):
-                run(sweep * T + RUN * i, base + sign * (RUN * i + 1), NG, sign)
-                return 0
-
-            def short(i, _):
-                run(sweep * T + RUN * i, base + (8 * DROP if sign < 0 else 0) + sign * (RUN * i + 1), NG - DROP, sign)
-                return 0
-
-            lax.fori_loop(0, half, full, 0)
-            lax.fori_loop(half, T // RUN, short, 0)
-
-        @pl.when(odd == 0)
-        def _():
-            steps(-1)
-
-        @pl.when(odd == 1)
-        def _():
-            steps(1)
+        for sign in (-1, 1):
+            for begins in (True, False):
+                @pl.when((2 * odd - 1 == sign) & ((c == 0) == begins))
+                def _():
+                    run(sweep * T, base, sign, begins)
 
         @pl.when(sweep == SWEEPS - 1)
         def _():
@@ -291,7 +286,7 @@
                 pltpu.VMEM((ROWS + 2 * T, COLS), F32), pltpu.VMEM((ROWS + 2 * T, COLS), F32),
                 pltpu.VMEM((2, ROWS, 128), F32), pltpu.VMEM((2, ROWS + 2 * T, 128), F32), pltpu.VMEM((2, G, TILE, 128), F32),
                 pltpu.VMEM((SWEEPS - 1, 2, G, T, 128), F32), pltpu.VMEM((SWEEPS - 1, 2, 2, G, T, 128), F32),
-                dma((2, 4)), dma((2, 2)), dma((2, 2)), dma((TILES,)), dma((TILES,)), dma((2,)), dma((2,)),
+                dma((2, 8)), dma((2, 2)), dma((2, 2)), dma((TILES,)), dma((TILES,)), dma((2,)), dma((2,)),
                 dma((SWEEPS - 1, 2)), dma((SWEEPS - 1, 2)),
             ],
             compiler_params=pltpu.CompilerParams(collective_id=0, has_side_effects=True, vmem_limit_bytes=VMEM_LIMIT),

time: 36.4 us -> 35.6 us (0.978)
  Pallas kernels: 34.6 us -> 33.8 us
    pallas_call x1, Pallas kernels: 34.6 us -> 33.8 us  [local_run(): pl.pallas_call(wave_kernel, out_shape=[jax.ShapeDtypeStruct((ROWS, COLS),...]
where the time goes in v7:
time: 35.6 us; the launch traced here: 35.5 us
  Pallas kernels  33.8 us (95%)
  other arithmetic  1.08 us (3%)
  between operations  0.64 us (2%)
    pallas_call x1, Pallas kernels, local_run(): pl.pallas_call(wave_kernel, out_shape=[jax.ShapeDtypeStruct((ROWS, COLS),...  33.8 us
    mul x1, other arithmetic, local_run(): return (4.0 * now, 8.0 * (now - before))  1.08 us

profile of v7, /device:TPU:0, one launch (start us, length us, event | category | flops | bytes accessed | tf_op | source)
XLA Modules:
  0.0 35.5 jit_solution(17344690712500135465)
XLA Ops:
  0.6 33.8 %shard_map.50 = (f32[256,512]{1,0:T(8,128)S(1)}, f32[256,512]{1,0:T(8,128)S(1)}) custom-call(f32[256,512]{1,0:T(8,128)} %u_hbm.1, f32[256,512]{1,0:T(8,128)} %v_hbm.1, f32[3,3,64]{2,1,0:T(4,128)} %bitcast.1), custom_call_target="tpu_custom_call" | custom-call | tf_op jit(solution)/shard_map/pallas_call | solution.py:279
  34.4 1.1 %subtract_multiply_fusion = (f32[256,512]{1,0:T(8,128)}, f32[256,512]{1,0:T(8,128)}) fusion(f32[256,512]{1,0:T(8,128)S(1)} %get-tuple-element.4, f32[256,512]{1,0:T(8,128)S(1)} %get-tuple-element.5), kind=kLoop, calls=%fused_computation | loop fusion | flops 393216 | bytes 2097152 | tf_op jit(solution)/shard_map/mul | solution.py:294

commit v8 on v7

--- a/solution.py
+++ b/solution.py
@@ -21,7 +21,7 @@
 
 
 def wave_kernel(u_hbm, v_hbm, w_hbm, now_ref, before_ref, st, w_ref, maps, uraw, vraw, pbuf, hbuf, zbuf, sbuf, rbuf,
-                load_sem, raw_ssem, raw_rsem, pk_ssem, pk_rsem, dg_ssem, dg_rsem, ex_ssem, ex_rsem):
+                load_sem, raw_ssem, raw_rsem, pk_ssem, pk_rsem, dg_rsem, ex_ssem, ex_rsem):
     row = lax.axis_index("row")
     col = lax.axis_index("col")
     up = lax.rem(row + 3, 4)
@@ -34,13 +34,21 @@
 
     cuts = [0] + [TILE * (c + 1) - T for c in range(TILES - 1)] + [ROWS]
 
-    pieces = [(lo, n, at, 128) for lo, n in ((ROWS - T, T), (0, cuts[1]), (cuts[1], ROWS - T - cuts[1])) for at in (0, COLS - 128)]
-    pieces.append((0, ROWS, 128, COLS - 256))
-    loads = [pltpu.make_async_copy(src.at[pl.ds(lo, n), pl.ds(at, m)], dst.at[pl.ds(T + lo, n), pl.ds(at, m)], load_sem.at[f, k])
-             for k, (lo, n, at, m) in enumerate(pieces) for f, (src, dst) in enumerate(((u_hbm, uraw), (v_hbm, vraw)))]
-    loads.append(pltpu.make_async_copy(w_hbm, w_ref, load_sem.at[0, len(pieces)]))
-    for cp in loads:
-        cp.start()
+    stages = [[(lo, n, at, 128) for lo, n in spans for at in (0, COLS - 128)]
+              for spans in (((ROWS - T, T), (0, cuts[1])), ((cuts[1], ROWS - T - cuts[1]),))]
+    stages.append([(0, ROWS, 128, COLS - 256)])
+    for k, pieces in enumerate(stages):
+        for lo, n, at, m in pieces:
+            for src, dst in ((u_hbm, uraw), (v_hbm, vraw)):
+                pltpu.make_async_copy(src.at[pl.ds(lo, n), pl.ds(at, m)], dst.at[pl.ds(T + lo, n), pl.ds(at, m)], load_sem.at[k]).start()
+    weights = pltpu.make_async_copy(w_hbm, w_ref, load_sem.at[3])
+    weights.start()
+
+    def wait_bytes(ref, sem):
+        pltpu.make_async_copy(ref, ref, sem).wait()
+
+    def wait_stage(k):
+        wait_bytes(uraw.at[pl.ds(0, sum(n * m for _, n, _, m in stages[k]) * 2 // COLS)], load_sem.at[k])
 
     def zero(i, _):
         for f in range(2):
@@ -66,7 +74,7 @@
         lo, at, to = ((0, T + ROWS, up), (ROWS - T, 0, down))[side]
         return pltpu.make_async_remote_copy(
             src_ref=src.at[pl.ds(lo, T)], dst_ref=dst.at[pl.ds(at, T)],
-            send_sem=raw_ssem.at[f, side], recv_sem=raw_rsem.at[f, side],
+            send_sem=raw_ssem.at[0], recv_sem=raw_rsem.at[side],
             device_id={"row": to, "col": col}, device_id_type=MESH)
 
     raws = [raw_copy(f, side) for side in range(2) for f in range(2)]
@@ -77,21 +85,20 @@
         n = cuts[c + 1] - cuts[c]
         return pltpu.make_async_remote_copy(
             src_ref=pbuf.at[:, pl.ds(cuts[c], n)], dst_ref=hbuf.at[:, pl.ds(T + cuts[c], n)],
-            send_sem=pk_ssem.at[c], recv_sem=pk_rsem.at[c],
+            send_sem=pk_ssem.at[0], recv_sem=pk_rsem.at[c],
             device_id={"row": row, "col": other}, device_id_type=MESH)
 
     def diag_copy(side):
         lo, at, to = ((0, T + ROWS, up), (ROWS - T, 0, down))[side]
         return pltpu.make_async_remote_copy(
             src_ref=pbuf.at[:, pl.ds(lo, T)], dst_ref=hbuf.at[:, pl.ds(at, T)],
-            send_sem=dg_ssem.at[side], recv_sem=dg_rsem.at[side],
+            send_sem=pk_ssem.at[0], recv_sem=dg_rsem.at[side],
             device_id={"row": to, "col": other}, device_id_type=MESH)
 
     packs = [packed_copy(c) for c in range(TILES)]
     diags = [diag_copy(side) for side in range(2)]
 
-    for cp in loads[:8]:
-        cp.wait()
+    wait_stage(0)
 
     def pack(i, _):
         r = pl.multiple_of(i * 8, 8)
@@ -104,14 +111,13 @@
     diags[1].start()
     packs[0].start()
     diags[0].start()
-    for cp in loads[8:12]:
-        cp.wait()
+    wait_stage(1)
     lax.fori_loop(cuts[1] // 8, (ROWS - T) // 8, pack, 0)
     packs[1].start()
     packs[2].start()
 
-    for cp in loads[12:]:
-        cp.wait()
+    wait_stage(2)
+    weights.wait()
 
     def lanes(x, idx):
         return jnp.take_along_axis(x, idx, axis=1, mode="promise_in_bounds")
@@ -166,7 +172,7 @@
         src = sbuf.at[e] if late else st.at[:, pl.ds(1, G), pl.ds(jnp.where(side == 0, OFF, OFF + ROWS - T), T)]
         return pltpu.make_async_remote_copy(
             src_ref=src, dst_ref=rbuf.at[e, side],
-            send_sem=ex_ssem.at[e, side], recv_sem=ex_rsem.at[e, side],
+            send_sem=ex_ssem.at[int(late)], recv_sem=ex_rsem.at[e, side],
             device_id={"row": to, "col": col}, device_id_type=MESH)
 
     def get(lo):
@@ -193,8 +199,8 @@
 
         @pl.when(it == 0)
         def _():
-            raws[2].wait_recv()
-            raws[3].wait_recv()
+            wait_bytes(uraw.at[pl.ds(0, 2 * T)], raw_rsem.at[1])
+            wait_bytes(uraw.at[pl.ds(0, 4 * T)], raw_ssem.at[0])
             diags[1].wait_recv()
             packs[0].wait_recv()
 
@@ -204,8 +210,7 @@
 
         @pl.when(it == 2)
         def _():
-            raws[0].wait_recv()
-            raws[1].wait_recv()
+            wait_bytes(uraw.at[pl.ds(0, 2 * T)], raw_rsem.at[0])
             diags[0].wait_recv()
             packs[2].wait_recv()
 
@@ -243,13 +248,16 @@
             put_rows(first)
             exchange(sweep - 1, first, to_first, True).start()
 
+        @pl.when((sweep > 0) & (c == 1))
+        def _():
+            exchange(sweep - 1, last, up, False).wait_send()
+
         @pl.when((sweep < SWEEPS - 1) & (c == 1))
         def _():
             exchange(sweep, first, to_first, False).start()
 
         @pl.when((sweep > 0) & (c == TILES - 1))
         def _():
-            exchange(sweep - 1, last, up, False).wait_send()
             exchange(sweep - 1, 1 - last, up, True).wait_recv()
             put_rows(last)
 
@@ -267,10 +275,8 @@
 
     lax.fori_loop(0, SWEEPS * TILES, tile, 0)
 
-    for cp in raws + packs + diags:
-        cp.wait_send()
-    for e in range(SWEEPS - 1):
-        exchange(e, (e + 1) % 2, up, True).wait_send()
+    wait_bytes(hbuf, pk_ssem.at[0])
+    wait_bytes(sbuf, ex_ssem.at[1])
 
 
 def solution(mesh):
@@ -286,8 +292,7 @@
                 pltpu.VMEM((ROWS + 2 * T, COLS), F32), pltpu.VMEM((ROWS + 2 * T, COLS), F32),
                 pltpu.VMEM((2, ROWS, 128), F32), pltpu.VMEM((2, ROWS + 2 * T, 128), F32), pltpu.VMEM((2, G, TILE, 128), F32),
                 pltpu.VMEM((SWEEPS - 1, 2, G, T, 128), F32), pltpu.VMEM((SWEEPS - 1, 2, 2, G, T, 128), F32),
-                dma((2, 8)), dma((2, 2)), dma((2, 2)), dma((TILES,)), dma((TILES,)), dma((2,)), dma((2,)),
-                dma((SWEEPS - 1, 2)), dma((SWEEPS - 1, 2)),
+                dma((4,)), dma((1,)), dma((2,)), dma((1,)), dma((TILES,)), dma((2,)), dma((2,)), dma((SWEEPS - 1, 2)),
             ],
             compiler_params=pltpu.CompilerParams(collective_id=0, has_side_effects=True, vmem_limit_bytes=VMEM_LIMIT),
         )(u_tile, v_tile, pltpu.with_memory_space_constraint(jnp.transpose(w, (1, 2, 0)), pltpu.HBM))

time: 35.6 us -> 35.3 us (level)
  no operation moved by 1% of the time
where the time goes in v8:
time: 35.3 us; the launch traced here: 35.2 us
  Pallas kernels  33.5 us (95%)
  other arithmetic  1.08 us (3%)
  between operations  0.64 us (2%)
    pallas_call x1, Pallas kernels, local_run(): pl.pallas_call(wave_kernel, out_shape=[jax.ShapeDtypeStruct((ROWS, COLS),...  33.5 us
    mul x1, other arithmetic, local_run(): return (4.0 * now, 8.0 * (now - before))  1.08 us

profile of v8, /device:TPU:0, one launch (start us, length us, event | category | flops | bytes accessed | tf_op | source)
XLA Modules:
  0.0 35.2 jit_solution(9753754333143402590)
XLA Ops:
  0.6 33.5 %shard_map.50 = (f32[256,512]{1,0:T(8,128)S(1)}, f32[256,512]{1,0:T(8,128)S(1)}) custom-call(f32[256,512]{1,0:T(8,128)} %u_hbm.1, f32[256,512]{1,0:T(8,128)} %v_hbm.1, f32[3,3,64]{2,1,0:T(4,128)} %bitcast.1), custom_call_target="tpu_custom_call" | custom-call | tf_op jit(solution)/shard_map/pallas_call | solution.py:285
  34.1 1.1 %subtract_multiply_fusion = (f32[256,512]{1,0:T(8,128)}, f32[256,512]{1,0:T(8,128)}) fusion(f32[256,512]{1,0:T(8,128)S(1)} %get-tuple-element.4, f32[256,512]{1,0:T(8,128)S(1)} %get-tuple-element.5), kind=kLoop, calls=%fused_computation | loop fusion | flops 393216 | bytes 2097152 | tf_op jit(solution)/shard_map/mul | solution.py:299

commit v9 on v8

--- a/solution.py
+++ b/solution.py
@@ -122,25 +122,50 @@
     def lanes(x, idx):
         return jnp.take_along_axis(x, idx, axis=1, mode="promise_in_bounds")
 
-    def put(c):
+    def put_main(c):
         residue = maps[2 * G]
         for g in range(G):
             idx = maps[g]
+            masks = [residue == (g + 1 + 2 * k) % G for k in range(3)]
             for n in range(NG):
                 r = pl.multiple_of(c * TILE + 8 * n, 8)
                 q = pl.multiple_of(c * TILE + (OFF - T + 8 * n), 8)
-                u, v = hbuf[0, pl.ds(r, 8), :], hbuf[1, pl.ds(r, 8), :]
-                for k in range(4):
-                    mask = residue == (g + 1 + 2 * k) % G
-                    u = jnp.where(mask, uraw[pl.ds(r, 8), 128 * k:128 * k + 128], u)
-                    v = jnp.where(mask, vraw[pl.ds(r, 8), 128 * k:128 * k + 128], v)
+                u, v = uraw[pl.ds(r, 8), 384:512], vraw[pl.ds(r, 8), 384:512]
+                for k in range(3):
+                    u = jnp.where(masks[k], uraw[pl.ds(r, 8), 128 * k:128 * k + 128], u)
+                    v = jnp.where(masks[k], vraw[pl.ds(r, 8), 128 * k:128 * k + 128], v)
                 x = 0.25 * lanes(u, idx)
                 st[0, g + 1, pl.ds(q, 8), :] = x
                 st[1, g + 1, pl.ds(q, 8), :] = x - 0.125 * lanes(v, idx)
-        for n in range(NG):
-            q = pl.multiple_of(c * TILE + (OFF - T + 8 * n), 8)
-            st[0, G + 1, pl.ds(q, 8), :] = pltpu.roll(st[0, 1, pl.ds(q, 8), :], 127, 1)
-            st[0, 0, pl.ds(q, 8), :] = pltpu.roll(st[0, G, pl.ds(q, 8), :], 1, 1)
+
+    def put_halo(c):
+        for g in range(G):
+            idx = maps[g]
+            column = lane * G + (g - 64)
+            halo = (column < 0) | (column >= COLS)
+            for n in range(NG):
+                r = pl.multiple_of(c * TILE + 8 * n, 8)
+                q = pl.multiple_of(c * TILE + (OFF - T + 8 * n), 8)
+                h = 0.25 * lanes(hbuf[0, pl.ds(r, 8), :], idx)
+                x = jnp.where(halo, h, st[0, g + 1, pl.ds(q, 8), :])
+                st[0, g + 1, pl.ds(q, 8), :] = x
+                st[1, g + 1, pl.ds(q, 8), :] = jnp.where(halo, h - 0.125 * lanes(hbuf[1, pl.ds(r, 8), :], idx), st[1, g + 1, pl.ds(q, 8), :])
+                if g == 0:
+                    st[0, G + 1, pl.ds(q, 8), :] = pltpu.roll(x, 127, 1)
+                if g == G - 1:
+                    st[0, 0, pl.ds(q, 8), :] = pltpu.roll(x, 1, 1)
+
+    def put_tile(i, _):
+        @pl.when(i == 1)
+        def _():
+            wait_bytes(uraw.at[pl.ds(0, 2 * T)], raw_rsem.at[1])
+            wait_bytes(uraw.at[pl.ds(0, 2 * T)], raw_rsem.at[0])
+            wait_bytes(uraw.at[pl.ds(0, 4 * T)], raw_ssem.at[0])
+
+        put_main(lax.rem(i + 1, TILES))
+        return 0
+
+    lax.fori_loop(0, TILES, put_tile, 0)
 
     def run(t, base, sign, first):
         drops = [2 * (k + 1) // 8 if first else 0 for k in range(T)]
@@ -199,8 +224,6 @@
 
         @pl.when(it == 0)
         def _():
-            wait_bytes(uraw.at[pl.ds(0, 2 * T)], raw_rsem.at[1])
-            wait_bytes(uraw.at[pl.ds(0, 4 * T)], raw_ssem.at[0])
             diags[1].wait_recv()
             packs[0].wait_recv()
 
@@ -210,13 +233,12 @@
 
         @pl.when(it == 2)
         def _():
-            wait_bytes(uraw.at[pl.ds(0, 2 * T)], raw_rsem.at[0])
             diags[0].wait_recv()
             packs[2].wait_recv()
 
         @pl.when(sweep == 0)
         def _():
-            put(c)
+            put_halo(c)
 
         first = odd
         last = 1 - odd

time: 35.3 us -> 35.2 us (level)
  no operation moved by 1% of the time
where the time goes in v9:
time: 35.2 us; the launch traced here: 35.1 us
  Pallas kernels  33.4 us (95%)
  other arithmetic  1.08 us (3%)
  between operations  0.64 us (2%)
    pallas_call x1, Pallas kernels, local_run(): pl.pallas_call(wave_kernel, out_shape=[jax.ShapeDtypeStruct((ROWS, COLS),...  33.4 us
    mul x1, other arithmetic, local_run(): return (4.0 * now, 8.0 * (now - before))  1.08 us

profile of v9, /device:TPU:0, one launch (start us, length us, event | category | flops | bytes accessed | tf_op | source)
XLA Modules:
  0.0 35.1 jit_solution(13272169308623928254)
XLA Ops:
  0.6 33.4 %shard_map.50 = (f32[256,512]{1,0:T(8,128)S(1)}, f32[256,512]{1,0:T(8,128)S(1)}) custom-call(f32[256,512]{1,0:T(8,128)} %u_hbm.1, f32[256,512]{1,0:T(8,128)} %v_hbm.1, f32[3,3,64]{2,1,0:T(4,128)} %bitcast.1), custom_call_target="tpu_custom_call" | custom-call | tf_op jit(solution)/shard_map/pallas_call | solution.py:307
  34.0 1.1 %subtract_multiply_fusion = (f32[256,512]{1,0:T(8,128)}, f32[256,512]{1,0:T(8,128)}) fusion(f32[256,512]{1,0:T(8,128)S(1)} %get-tuple-element.4, f32[256,512]{1,0:T(8,128)S(1)} %get-tuple-element.5), kind=kLoop, calls=%fused_computation | loop fusion | flops 393216 | bytes 2097152 | tf_op jit(solution)/shard_map/mul | solution.py:321

commit v10 on v9

--- a/solution.py
+++ b/solution.py
@@ -139,21 +139,22 @@
                 st[1, g + 1, pl.ds(q, 8), :] = x - 0.125 * lanes(v, idx)
 
     def put_halo(c):
+        sv = st.at[:, :, pl.ds(pl.multiple_of(c * TILE + (OFF - T), 8), TILE)]
+        hv = hbuf.at[:, pl.ds(pl.multiple_of(c * TILE, 8), TILE)]
         for g in range(G):
             idx = maps[g]
             column = lane * G + (g - 64)
             halo = (column < 0) | (column >= COLS)
             for n in range(NG):
-                r = pl.multiple_of(c * TILE + 8 * n, 8)
-                q = pl.multiple_of(c * TILE + (OFF - T + 8 * n), 8)
-                h = 0.25 * lanes(hbuf[0, pl.ds(r, 8), :], idx)
-                x = jnp.where(halo, h, st[0, g + 1, pl.ds(q, 8), :])
-                st[0, g + 1, pl.ds(q, 8), :] = x
-                st[1, g + 1, pl.ds(q, 8), :] = jnp.where(halo, h - 0.125 * lanes(hbuf[1, pl.ds(r, 8), :], idx), st[1, g + 1, pl.ds(q, 8), :])
+                rows = pl.ds(8 * n, 8)
+                h = 0.25 * lanes(hv[0, rows, :], idx)
+                x = jnp.where(halo, h, sv[0, g + 1, rows, :])
+                sv[0, g + 1, rows, :] = x
+                sv[1, g + 1, rows, :] = jnp.where(halo, h - 0.125 * lanes(hv[1, rows, :], idx), sv[1, g + 1, rows, :])
                 if g == 0:
-                    st[0, G + 1, pl.ds(q, 8), :] = pltpu.roll(x, 127, 1)
+                    sv[0, G + 1, rows, :] = pltpu.roll(x, 127, 1)
                 if g == G - 1:
-                    st[0, 0, pl.ds(q, 8), :] = pltpu.roll(x, 1, 1)
+                    sv[0, 0, rows, :] = pltpu.roll(x, 1, 1)
 
     def put_tile(i, _):
         @pl.when(i == 1)

time: 35.2 us -> 35.2 us (level)
  no operation moved by 1% of the time
where the time goes in v10:
time: 35.2 us; the launch traced here: 35.1 us
  Pallas kernels  33.4 us (95%)
  other arithmetic  1.08 us (3%)
  between operations  0.64 us (2%)
    pallas_call x1, Pallas kernels, local_run(): pl.pallas_call(wave_kernel, out_shape=[jax.ShapeDtypeStruct((ROWS, COLS),...  33.4 us
    mul x1, other arithmetic, local_run(): return (4.0 * now, 8.0 * (now - before))  1.08 us

profile of v10, /device:TPU:0, one launch (start us, length us, event | category | flops | bytes accessed | tf_op | source)
XLA Modules:
  0.0 35.1 jit_solution(13272169308623928254)
XLA Ops:
  0.6 33.4 %shard_map.50 = (f32[256,512]{1,0:T(8,128)S(1)}, f32[256,512]{1,0:T(8,128)S(1)}) custom-call(f32[256,512]{1,0:T(8,128)} %u_hbm.1, f32[256,512]{1,0:T(8,128)} %v_hbm.1, f32[3,3,64]{2,1,0:T(4,128)} %bitcast.1), custom_call_target="tpu_custom_call" | custom-call | tf_op jit(solution)/shard_map/pallas_call | solution.py:308
  34.0 1.1 %subtract_multiply_fusion = (f32[256,512]{1,0:T(8,128)}, f32[256,512]{1,0:T(8,128)}) fusion(f32[256,512]{1,0:T(8,128)S(1)} %get-tuple-element.4, f32[256,512]{1,0:T(8,128)S(1)} %get-tuple-element.5), kind=kLoop, calls=%fused_computation | loop fusion | flops 393216 | bytes 2097152 | tf_op jit(solution)/shard_map/mul | solution.py:322

commit v11 on v10

--- a/solution.py
+++ b/solution.py
@@ -15,6 +15,8 @@
 TILE = (ROWS + 2 * T) // TILES
 NG = TILE // 8
 BLOCK = 4
+EARLY = 8
+ORDER_STEPS = (1, 3, 5, 7, 9)
 OFF = 32
 R = 328
 VMEM_LIMIT = 55_300_000
@@ -168,11 +170,32 @@
 
     lax.fori_loop(0, TILES, put_tile, 0)
 
-    def run(t, base, sign, first):
+    def merge(lo, groups):
+        residue = maps[2 * G]
+        for f, out in ((0, now_ref), (1, before_ref)):
+            ov = out.at[pl.ds(lo, 8 * groups)]
+            for n in range(groups):
+                for k in range(4):
+                    x = zbuf[f, 0, 8 * n:8 * n + 8, :]
+                    for g in range(1, G):
+                        x = jnp.where(residue == (g + 1 + 2 * k) % G, zbuf[f, g, 8 * n:8 * n + 8, :], x)
+                    ov[8 * n:8 * n + 8, 128 * k:128 * k + 128] = x
+
+    def get(lo, groups):
+        for g in range(G):
+            for n in range(groups):
+                for f in range(2):
+                    zbuf[f, g, 8 * n:8 * n + 8, :] = lanes(st[f, g + 1, pl.ds(lo + OFF + 8 * n, 8), :], maps[G + g])
+        merge(lo, groups)
+
+    def run(t, base, sign, first, lo=None):
         drops = [2 * (k + 1) // 8 if first else 0 for k in range(T)]
         tops = [sign * (k + 1) + (8 * drops[k] if sign < 0 else 0) for k in range(T)]
         low = min(tops) - 1
         high = max(top + TILE - 8 * drop for top, drop in zip(tops, drops)) + 1
+        done = TILE + T
+        if lo is not None:
+            high = max(high, done + 8 * EARLY)
         sv = st.at[:, :, pl.ds(base + low, high - low)]
         for k in range(T):
             src, dst = k % 2, 1 - k % 2
@@ -193,6 +216,13 @@
                 sv[dst, 1:G + 1, pl.ds(q, rows), :] = x
                 sv[dst, G + 1, pl.ds(q, rows), :] = pltpu.roll(x[0], 127, 1)
                 sv[dst, 0, pl.ds(q, rows), :] = pltpu.roll(x[G - 1], 1, 1)
+            if lo is not None and k in ORDER_STEPS:
+                g = ORDER_STEPS.index(k)
+                for n in range(EARLY):
+                    for f in range(2):
+                        zbuf[f, g, 8 * n:8 * n + 8, :] = lanes(sv[f, g + 1, pl.ds(done - low + 8 * n, 8), :], maps[G + g])
+        if lo is not None:
+            merge(lo, EARLY)
 
     def exchange(e, side, to, late):
         src = sbuf.at[e] if late else st.at[:, pl.ds(1, G), pl.ds(jnp.where(side == 0, OFF, OFF + ROWS - T), T)]
@@ -200,23 +230,6 @@
             src_ref=src, dst_ref=rbuf.at[e, side],
             send_sem=ex_ssem.at[int(late)], recv_sem=ex_rsem.at[e, side],
             device_id={"row": to, "col": col}, device_id_type=MESH)
-
-    def get(lo):
-        for g in range(G):
-            idx = maps[G + g]
-            for n in range(NG):
-                q = pl.multiple_of(lo + (OFF + 8 * n), 8)
-                for f in range(2):
-                    zbuf[f, g, 8 * n:8 * n + 8, :] = lanes(st[f, g + 1, pl.ds(q, 8), :], idx)
-        residue = maps[2 * G]
-        for n in range(NG):
-            r = pl.multiple_of(lo + 8 * n, 8)
-            for f, out in ((0, now_ref), (1, before_ref)):
-                for k in range(4):
-                    x = zbuf[f, 0, 8 * n:8 * n + 8, :]
-                    for g in range(1, G):
-                        x = jnp.where(residue == (g + 1 + 2 * k) % G, zbuf[f, g, 8 * n:8 * n + 8, :], x)
-                    out[pl.ds(r, 8), 128 * k:128 * k + 128] = x
 
     def tile(it, _):
         sweep, c = lax.div(it, TILES), lax.rem(it, TILES)
@@ -286,17 +299,19 @@
 
         for sign in (-1, 1):
             for begins in (True, False):
-                @pl.when((2 * odd - 1 == sign) & ((c == 0) == begins))
+                @pl.when((2 * odd - 1 == sign) & ((c == 0) == begins) & ((sweep < SWEEPS - 1) | begins))
                 def _():
                     run(sweep * T, base, sign, begins)
 
-        @pl.when(sweep == SWEEPS - 1)
-        def _():
-            get(pl.multiple_of(jnp.where(c == 0, ROWS - TILE, (TILES - 1 - c) * TILE), 8))
+        @pl.when((sweep == SWEEPS - 1) & (c > 0))
+        def _():
+            run(sweep * T, base, 1, False, pl.multiple_of(ROWS + 2 * T - TILE * c, 8))
 
         return 0
 
     lax.fori_loop(0, SWEEPS * TILES, tile, 0)
+    get(0, NG)
+    get(ROWS + 2 * T - 2 * TILE + 8 * EARLY, NG - EARLY)
 
     wait_bytes(hbuf, pk_ssem.at[0])
     wait_bytes(sbuf, ex_ssem.at[1])

time: 35.2 us -> 35.3 us (level)
  no operation moved by 1% of the time
where the time goes in v11:
time: 35.3 us; the launch traced here: 35.2 us
  Pallas kernels  33.4 us (95%)
  other arithmetic  1.08 us (3%)
  between operations  0.64 us (2%)
    pallas_call x1, Pallas kernels, local_run(): pl.pallas_call(wave_kernel, out_shape=[jax.ShapeDtypeStruct((ROWS, COLS),...  33.4 us
    mul x1, other arithmetic, local_run(): return (4.0 * now, 8.0 * (now - before))  1.08 us

profile of v11, /device:TPU:0, one launch (start us, length us, event | category | flops | bytes accessed | tf_op | source)
XLA Modules:
  0.0 35.2 jit_solution(9611026590807934569)
XLA Ops:
  0.6 33.4 %shard_map.50 = (f32[256,512]{1,0:T(8,128)S(1)}, f32[256,512]{1,0:T(8,128)S(1)}) custom-call(f32[256,512]{1,0:T(8,128)} %u_hbm.1, f32[256,512]{1,0:T(8,128)} %v_hbm.1, f32[3,3,64]{2,1,0:T(4,128)} %bitcast.1), custom_call_target="tpu_custom_call" | custom-call | tf_op jit(solution)/shard_map/pallas_call | solution.py:323
  34.1 1.1 %subtract_multiply_fusion = (f32[256,512]{1,0:T(8,128)}, f32[256,512]{1,0:T(8,128)}) fusion(f32[256,512]{1,0:T(8,128)S(1)} %get-tuple-element.4, f32[256,512]{1,0:T(8,128)S(1)} %get-tuple-element.5), kind=kLoop, calls=%fused_computation | loop fusion | flops 393216 | bytes 2097152 | tf_op jit(solution)/shard_map/mul | solution.py:337

commit v12 on v10

--- a/solution.py
+++ b/solution.py
@@ -32,15 +32,19 @@
     for rr, cc in ((row, other), (up, col), (down, col), (up, other), (down, other)):
         pl.semaphore_signal(barrier, inc=1, device_id={"row": rr, "col": cc}, device_id_type=MESH)
 
-    cuts = [0] + [TILE * (c + 1) - T for c in range(TILES - 1)] + [ROWS]
+    cuts = [0, TILE // 2 - T] + [TILE * (c + 1) - T for c in range(TILES - 1)] + [ROWS]
 
     stages = [[(lo, n, at, 128) for lo, n in spans for at in (0, COLS - 128)]
-              for spans in (((ROWS - T, T), (0, cuts[1])), ((cuts[1], ROWS - T - cuts[1]),))]
+              for spans in (((ROWS - T, T), (0, cuts[2])), ((cuts[2], ROWS - T - cuts[2]),))]
     stages.append([(0, ROWS, 128, COLS - 256)])
-    for k, pieces in enumerate(stages):
-        for lo, n, at, m in pieces:
+
+    def start_stage(k):
+        for lo, n, at, m in stages[k]:
             for src, dst in ((u_hbm, uraw), (v_hbm, vraw)):
                 pltpu.make_async_copy(src.at[pl.ds(lo, n), pl.ds(at, m)], dst.at[pl.ds(T + lo, n), pl.ds(at, m)], load_sem.at[k]).start()
+
+    start_stage(0)
+    start_stage(1)
     weights = pltpu.make_async_copy(w_hbm, w_ref, load_sem.at[3])
     weights.start()
 
@@ -95,10 +99,11 @@
             send_sem=pk_ssem.at[0], recv_sem=dg_rsem.at[side],
             device_id={"row": to, "col": other}, device_id_type=MESH)
 
-    packs = [packed_copy(c) for c in range(TILES)]
+    packs = [packed_copy(c) for c in range(TILES + 1)]
     diags = [diag_copy(side) for side in range(2)]
 
     wait_stage(0)
+    start_stage(2)
 
     def pack(i, _):
         r = pl.multiple_of(i * 8, 8)
@@ -107,14 +112,15 @@
         return 0
 
     lax.fori_loop((ROWS - T) // 8, ROWS // 8, pack, 0)
-    lax.fori_loop(0, cuts[1] // 8, pack, 0)
+    lax.fori_loop(0, cuts[2] // 8, pack, 0)
     diags[1].start()
     packs[0].start()
+    packs[1].start()
     diags[0].start()
     wait_stage(1)
-    lax.fori_loop(cuts[1] // 8, (ROWS - T) // 8, pack, 0)
-    packs[1].start()
+    lax.fori_loop(cuts[2] // 8, (ROWS - T) // 8, pack, 0)
     packs[2].start()
+    packs[3].start()
 
     wait_stage(2)
     weights.wait()
@@ -138,14 +144,14 @@
                 st[0, g + 1, pl.ds(q, 8), :] = x
                 st[1, g + 1, pl.ds(q, 8), :] = x - 0.125 * lanes(v, idx)
 
-    def put_halo(c):
-        sv = st.at[:, :, pl.ds(pl.multiple_of(c * TILE + (OFF - T), 8), TILE)]
-        hv = hbuf.at[:, pl.ds(pl.multiple_of(c * TILE, 8), TILE)]
+    def put_halo(at, groups):
+        sv = st.at[:, :, pl.ds(at + (OFF - T), 8 * groups)]
+        hv = hbuf.at[:, pl.ds(at, 8 * groups)]
         for g in range(G):
             idx = maps[g]
             column = lane * G + (g - 64)
             halo = (column < 0) | (column >= COLS)
-            for n in range(NG):
+            for n in range(groups):
                 rows = pl.ds(8 * n, 8)
                 h = 0.25 * lanes(hv[0, rows, :], idx)
                 x = jnp.where(halo, h, sv[0, g + 1, rows, :])
@@ -227,19 +233,22 @@
         def _():
             diags[1].wait_recv()
             packs[0].wait_recv()
+            put_halo(0, NG // 2)
+            packs[1].wait_recv()
+            put_halo(TILE // 2, NG // 2)
 
         @pl.when(it == 1)
         def _():
-            packs[1].wait_recv()
+            packs[2].wait_recv()
 
         @pl.when(it == 2)
         def _():
             diags[0].wait_recv()
-            packs[2].wait_recv()
-
-        @pl.when(sweep == 0)
-        def _():
-            put_halo(c)
+            packs[3].wait_recv()
+
+        @pl.when((sweep == 0) & (c > 0))
+        def _():
+            put_halo(pl.multiple_of(c * TILE, 8), NG)
 
         first = odd
         last = 1 - odd
@@ -315,7 +324,7 @@
                 pltpu.VMEM((ROWS + 2 * T, COLS), F32), pltpu.VMEM((ROWS + 2 * T, COLS), F32),
                 pltpu.VMEM((2, ROWS, 128), F32), pltpu.VMEM((2, ROWS + 2 * T, 128), F32), pltpu.VMEM((2, G, TILE, 128), F32),
                 pltpu.VMEM((SWEEPS - 1, 2, G, T, 128), F32), pltpu.VMEM((SWEEPS - 1, 2, 2, G, T, 128), F32),
-                dma((4,)), dma((1,)), dma((2,)), dma((1,)), dma((TILES,)), dma((2,)), dma((2,)), dma((SWEEPS - 1, 2)),
+                dma((4,)), dma((1,)), dma((2,)), dma((1,)), dma((TILES + 1,)), dma((2,)), dma((2,)), dma((SWEEPS - 1, 2)),
             ],
             compiler_params=pltpu.CompilerParams(collective_id=0, has_side_effects=True, vmem_limit_bytes=VMEM_LIMIT),
         )(u_tile, v_tile, pltpu.with_memory_space_constraint(jnp.transpose(w, (1, 2, 0)), pltpu.HBM))

time: 35.2 us -> 35.3 us (level)
  no operation moved by 1% of the time
where the time goes in v12:
time: 35.3 us; the launch traced here: 35.1 us
  Pallas kernels  33.4 us (95%)
  other arithmetic  1.08 us (3%)
  between operations  0.64 us (2%)
    pallas_call x1, Pallas kernels, local_run(): pl.pallas_call(wave_kernel, out_shape=[jax.ShapeDtypeStruct((ROWS, COLS),...  33.4 us
    mul x1, other arithmetic, local_run(): return (4.0 * now, 8.0 * (now - before))  1.08 us

profile of v12, /device:TPU:0, one launch (start us, length us, event | category | flops | bytes accessed | tf_op | source)
XLA Modules:
  0.0 35.1 jit_solution(16843837951375888018)
XLA Ops:
  0.6 33.4 %shard_map.50 = (f32[256,512]{1,0:T(8,128)S(1)}, f32[256,512]{1,0:T(8,128)S(1)}) custom-call(f32[256,512]{1,0:T(8,128)} %u_hbm.1, f32[256,512]{1,0:T(8,128)} %v_hbm.1, f32[3,3,64]{2,1,0:T(4,128)} %bitcast.1), custom_call_target="tpu_custom_call" | custom-call | tf_op jit(solution)/shard_map/pallas_call | solution.py:317
  34.0 1.1 %subtract_multiply_fusion = (f32[256,512]{1,0:T(8,128)}, f32[256,512]{1,0:T(8,128)}) fusion(f32[256,512]{1,0:T(8,128)S(1)} %get-tuple-element.4, f32[256,512]{1,0:T(8,128)S(1)} %get-tuple-element.5), kind=kLoop, calls=%fused_computation | loop fusion | flops 393216 | bytes 2097152 | tf_op jit(solution)/shard_map/mul | solution.py:331

commit v13 on v12

--- a/solution.py
+++ b/solution.py
@@ -116,10 +116,10 @@
     diags[1].start()
     packs[0].start()
     packs[1].start()
-    diags[0].start()
     wait_stage(1)
     lax.fori_loop(cuts[2] // 8, (ROWS - T) // 8, pack, 0)
     packs[2].start()
+    diags[0].start()
     packs[3].start()
 
     wait_stage(2)

time: 35.3 us -> 35.3 us (level)
  no operation moved by 1% of the time
where the time goes in v13:
time: 35.3 us; the launch traced here: 35.1 us
  Pallas kernels  33.4 us (95%)
  other arithmetic  1.08 us (3%)
  between operations  0.64 us (2%)
    pallas_call x1, Pallas kernels, local_run(): pl.pallas_call(wave_kernel, out_shape=[jax.ShapeDtypeStruct((ROWS, COLS),...  33.4 us
    mul x1, other arithmetic, local_run(): return (4.0 * now, 8.0 * (now - before))  1.08 us

profile of v13, /device:TPU:0, one launch (start us, length us, event | category | flops | bytes accessed | tf_op | source)
XLA Modules:
  0.0 35.1 jit_solution(8592830211408941993)
XLA Ops:
  0.6 33.4 %shard_map.50 = (f32[256,512]{1,0:T(8,128)S(1)}, f32[256,512]{1,0:T(8,128)S(1)}) custom-call(f32[256,512]{1,0:T(8,128)} %u_hbm.1, f32[256,512]{1,0:T(8,128)} %v_hbm.1, f32[3,3,64]{2,1,0:T(4,128)} %bitcast.1), custom_call_target="tpu_custom_call" | custom-call | tf_op jit(solution)/shard_map/pallas_call | solution.py:317
  34.0 1.1 %subtract_multiply_fusion = (f32[256,512]{1,0:T(8,128)}, f32[256,512]{1,0:T(8,128)}) fusion(f32[256,512]{1,0:T(8,128)S(1)} %get-tuple-element.4, f32[256,512]{1,0:T(8,128)S(1)} %get-tuple-element.5), kind=kLoop, calls=%fused_computation | loop fusion | flops 393216 | bytes 2097152 | tf_op jit(solution)/shard_map/mul | solution.py:331

commit v14 on v10

--- a/solution.py
+++ b/solution.py
@@ -21,7 +21,7 @@
 
 
 def wave_kernel(u_hbm, v_hbm, w_hbm, now_ref, before_ref, st, w_ref, maps, uraw, vraw, pbuf, hbuf, zbuf, sbuf, rbuf,
-                load_sem, raw_ssem, raw_rsem, pk_ssem, pk_rsem, dg_rsem, ex_ssem, ex_rsem):
+                load_sem, raw_rsem, pk_ssem, pk_rsem, dg_rsem, ex_rsem):
     row = lax.axis_index("row")
     col = lax.axis_index("col")
     up = lax.rem(row + 3, 4)
@@ -29,7 +29,7 @@
     other = 1 - col
 
     barrier = pltpu.get_barrier_semaphore()
-    for rr, cc in ((row, other), (up, col), (down, col), (up, other), (down, other)):
+    for rr, cc in ((up, other), (down, other), (row, other), (up, col), (down, col)):
         pl.semaphore_signal(barrier, inc=1, device_id={"row": rr, "col": cc}, device_id_type=MESH)
 
     cuts = [0] + [TILE * (c + 1) - T for c in range(TILES - 1)] + [ROWS]
@@ -74,7 +74,7 @@
         lo, at, to = ((0, T + ROWS, up), (ROWS - T, 0, down))[side]
         return pltpu.make_async_remote_copy(
             src_ref=src.at[pl.ds(lo, T)], dst_ref=dst.at[pl.ds(at, T)],
-            send_sem=raw_ssem.at[0], recv_sem=raw_rsem.at[side],
+            send_sem=pk_ssem.at[0], recv_sem=raw_rsem.at[side],
             device_id={"row": to, "col": col}, device_id_type=MESH)
 
     raws = [raw_copy(f, side) for side in range(2) for f in range(2)]
@@ -110,10 +110,10 @@
     lax.fori_loop(0, cuts[1] // 8, pack, 0)
     diags[1].start()
     packs[0].start()
-    diags[0].start()
     wait_stage(1)
     lax.fori_loop(cuts[1] // 8, (ROWS - T) // 8, pack, 0)
     packs[1].start()
+    diags[0].start()
     packs[2].start()
 
     wait_stage(2)
@@ -161,7 +161,6 @@
         def _():
             wait_bytes(uraw.at[pl.ds(0, 2 * T)], raw_rsem.at[1])
             wait_bytes(uraw.at[pl.ds(0, 2 * T)], raw_rsem.at[0])
-            wait_bytes(uraw.at[pl.ds(0, 4 * T)], raw_ssem.at[0])
 
         put_main(lax.rem(i + 1, TILES))
         return 0
@@ -198,7 +197,7 @@
         src = sbuf.at[e] if late else st.at[:, pl.ds(1, G), pl.ds(jnp.where(side == 0, OFF, OFF + ROWS - T), T)]
         return pltpu.make_async_remote_copy(
             src_ref=src, dst_ref=rbuf.at[e, side],
-            send_sem=ex_ssem.at[int(late)], recv_sem=ex_rsem.at[e, side],
+            send_sem=load_sem.at[int(late)], recv_sem=ex_rsem.at[e, side],
             device_id={"row": to, "col": col}, device_id_type=MESH)
 
     def get(lo):
@@ -298,8 +297,8 @@
 
     lax.fori_loop(0, SWEEPS * TILES, tile, 0)
 
-    wait_bytes(hbuf, pk_ssem.at[0])
-    wait_bytes(sbuf, ex_ssem.at[1])
+    wait_bytes(uraw.at[pl.ds(0, 4 * T + 2 * (ROWS + 2 * T) * 128 // COLS)], pk_ssem.at[0])
+    wait_bytes(sbuf, load_sem.at[1])
 
 
 def solution(mesh):
@@ -315,7 +314,7 @@
                 pltpu.VMEM((ROWS + 2 * T, COLS), F32), pltpu.VMEM((ROWS + 2 * T, COLS), F32),
                 pltpu.VMEM((2, ROWS, 128), F32), pltpu.VMEM((2, ROWS + 2 * T, 128), F32), pltpu.VMEM((2, G, TILE, 128), F32),
                 pltpu.VMEM((SWEEPS - 1, 2, G, T, 128), F32), pltpu.VMEM((SWEEPS - 1, 2, 2, G, T, 128), F32),
-                dma((4,)), dma((1,)), dma((2,)), dma((1,)), dma((TILES,)), dma((2,)), dma((2,)), dma((SWEEPS - 1, 2)),
+                dma((4,)), dma((2,)), dma((1,)), dma((TILES,)), dma((2,)), dma((SWEEPS - 1, 2)),
             ],
             compiler_params=pltpu.CompilerParams(collective_id=0, has_side_effects=True, vmem_limit_bytes=VMEM_LIMIT),
         )(u_tile, v_tile, pltpu.with_memory_space_constraint(jnp.transpose(w, (1, 2, 0)), pltpu.HBM))

time: 35.2 us -> 35.2 us (level)
  no operation moved by 1% of the time
where the time goes in v14:
time: 35.2 us; the launch traced here: 35.1 us
  Pallas kernels  33.4 us (95%)
  other arithmetic  1.08 us (3%)
  between operations  0.64 us (2%)
    pallas_call x1, Pallas kernels, local_run(): pl.pallas_call(wave_kernel, out_shape=[jax.ShapeDtypeStruct((ROWS, COLS),...  33.4 us
    mul x1, other arithmetic, local_run(): return (4.0 * now, 8.0 * (now - before))  1.08 us

profile of v14, /device:TPU:0, one launch (start us, length us, event | category | flops | bytes accessed | tf_op | source)
XLA Modules:
  0.0 35.1 jit_solution(14151601800555842689)
XLA Ops:
  0.6 33.4 %shard_map.50 = (f32[256,512]{1,0:T(8,128)S(1)}, f32[256,512]{1,0:T(8,128)S(1)}) custom-call(f32[256,512]{1,0:T(8,128)} %u_hbm.1, f32[256,512]{1,0:T(8,128)} %v_hbm.1, f32[3,3,64]{2,1,0:T(4,128)} %bitcast.1), custom_call_target="tpu_custom_call" | custom-call | tf_op jit(solution)/shard_map/pallas_call | solution.py:307
  34.0 1.1 %subtract_multiply_fusion = (f32[256,512]{1,0:T(8,128)}, f32[256,512]{1,0:T(8,128)}) fusion(f32[256,512]{1,0:T(8,128)S(1)} %get-tuple-element.4, f32[256,512]{1,0:T(8,128)S(1)} %get-tuple-element.5), kind=kLoop, calls=%fused_computation | loop fusion | flops 393216 | bytes 2097152 | tf_op jit(solution)/shard_map/mul | solution.py:321

commit v15 on v14

--- a/solution.py
+++ b/solution.py
@@ -14,7 +14,7 @@
 TILES = 3
 TILE = (ROWS + 2 * T) // TILES
 NG = TILE // 8
-BLOCK = 4
+BLOCK = 3
 OFF = 32
 R = 328
 VMEM_LIMIT = 55_300_000

time: 35.2 us -> 34.9 us (level)
  no operation moved by 1% of the time
where the time goes in v15:
time: 34.9 us; the launch traced here: 34.8 us
  Pallas kernels  33.1 us (95%)
  other arithmetic  1.08 us (3%)
  between operations  0.64 us (2%)
    pallas_call x1, Pallas kernels, local_run(): pl.pallas_call(wave_kernel, out_shape=[jax.ShapeDtypeStruct((ROWS, COLS),...  33.1 us
    mul x1, other arithmetic, local_run(): return (4.0 * now, 8.0 * (now - before))  1.08 us

profile of v15, /device:TPU:0, one launch (start us, length us, event | category | flops | bytes accessed | tf_op | source)
XLA Modules:
  0.0 34.8 jit_solution(3836067531101500132)
XLA Ops:
  0.6 33.1 %shard_map.50 = (f32[256,512]{1,0:T(8,128)S(1)}, f32[256,512]{1,0:T(8,128)S(1)}) custom-call(f32[256,512]{1,0:T(8,128)} %u_hbm.1, f32[256,512]{1,0:T(8,128)} %v_hbm.1, f32[3,3,64]{2,1,0:T(4,128)} %bitcast.1), custom_call_target="tpu_custom_call" | custom-call | tf_op jit(solution)/shard_map/pallas_call | solution.py:307
  33.7 1.1 %subtract_multiply_fusion = (f32[256,512]{1,0:T(8,128)}, f32[256,512]{1,0:T(8,128)}) fusion(f32[256,512]{1,0:T(8,128)S(1)} %get-tuple-element.4, f32[256,512]{1,0:T(8,128)S(1)} %get-tuple-element.5), kind=kLoop, calls=%fused_computation | loop fusion | flops 393216 | bytes 2097152 | tf_op jit(solution)/shard_map/mul | solution.py:321
